TPU v7x, 32 devices: a whole 2x2x4 slice. The times are simulated.
32 devices in a mesh: rve: 4 (over z), mic: 4 (over y, x), mac: 2 (over core).
Axes of the slice: x: 2, y: 2, z: 4, core: 2. Of those that a mesh axis runs over, the one named last changes fastest.
Arguments:
- displacement: float32 [3, 4, 8, 8], P(None, 'rve', ('mic', 'mac')), may hold values from -3 to 3
- plastic: float32 [256, 6, 16, 256], P(('rve', 'mic', 'mac')), may hold values from -0.3 to 0.3
- bulk_modulus: float32 [16, 256], replicated, may hold values from 1 to 3
- shear_modulus: float32 [16, 256], replicated, may hold values from 0.5 to 1.5
- yield_radius: float32 [16, 256], replicated, may hold values from 0.05 to 0.3
- counts: int32 [256], P(('rve', 'mic', 'mac')), may hold values from 0 to 3
- migration_plan: int32 [256], P(('rve', 'mic', 'mac')), may hold values from 0 to 255, as said below
Outputs:
- nodal_force: float32 [3, 4, 8, 8], P(None, 'rve', ('mic', 'mac'))
- plastic_new: float32 [256, 6, 16, 256], P(('rve', 'mic', 'mac'))
Inputs may be any that keep to these rules, and one draw needn't show every extreme that they name: migration_plan is a permutation of 0 .. 255. It keeps an RVE within the devices that share its mic and mac index; each device sends exactly 4 of its RVEs to each of 2 devices along rve and none to the others, so that every device receives 8. At each receiving device the RVEs are placed in order of rising iteration count.
All inputs are finite; a program needn't handle non-finite values.
Results may differ from a plain program's by a relative error of at most 0.0003.
Values sent between devices are 32-bit elements; how exact they have to be, the bound alone decides.
No kernel may reach another device: no remote copies, remote signals or barrier semaphores. Data moves between devices by JAX's collectives and lax.ppermute only.
A program may use at most 128 MiB of HBM per device.

v0:
```python
import math

import jax
import jax.numpy as jnp
import numpy as np
from jax import lax
from jax.experimental import pallas as pl
from jax.experimental.pallas import tpu as pltpu
from jax.sharding import PartitionSpec as P


COUPLING = 0.7
EARLY = 2
VMEM_BYTES = 48 * 2**20
PAIRS = [(0, 0), (1, 1), (2, 2), (1, 2), (0, 2), (0, 1)]
SYM = [(m, n) for m in range(6) for n in range(m, 6)]


def symbol_table(extent):
    wave = ((np.arange(extent) + extent // 2) % extent - extent // 2).astype(np.float64)
    grid = np.meshgrid(wave, wave, wave, indexing="ij")
    square = grid[0] ** 2 + grid[1] ** 2 + grid[2] ** 2
    live = square > 0
    safe = np.where(live, square, 1.0)
    full = np.zeros((6, 6) + square.shape)
    for n, (p, q) in enumerate(PAIRS):
        traction = [np.zeros_like(square) for _ in range(3)]
        traction[p] = traction[p] + grid[q]
        if p != q:
            traction[q] = traction[q] + grid[p]
        normal = sum(grid[i] * traction[i] for i in range(3))
        weight = 1.0 if p == q else 2.0
        for m, (i, j) in enumerate(PAIRS):
            value = (grid[j] * traction[i] + grid[i] * traction[j]) / (2.0 * safe)
            value = value - COUPLING * grid[i] * grid[j] * normal / safe**2
            full[m, n] = np.where(live, value, 0.0) / weight
    flip = (-np.arange(extent)) % extent
    mirrored = full[:, :, flip][:, :, :, flip][:, :, :, :, flip]
    real = 0.5 * (full + mirrored) / extent**3
    half = extent // 2
    scale = np.where((np.arange(half + 1) % half) == 0, 1.0, 2.0).reshape(-1, 1)
    table = np.zeros((len(SYM), extent, extent * extent))
    for index, (m, n) in enumerate(SYM):
        table[index, : half + 1] = real[m, n, : half + 1].reshape(half + 1, -1) * scale
    return table.astype(np.float32)


def plane_tables(extent):
    plane = np.arange(extent * extent)
    row, col = plane // extent, plane % extent
    phase = (row[:, None] * row[None, :] + col[:, None] * col[None, :]) % extent
    angle = 2.0 * np.pi * phase / extent
    out = []
    for value in (np.cos(angle) + np.sin(angle), np.cos(angle) - np.sin(angle)):
        value = value.astype(np.float32)
        high = value.astype(jnp.bfloat16)
        low = (value - high.astype(np.float32)).astype(jnp.bfloat16)
        out.append(np.concatenate([high, high, low], axis=0))
    return np.stack(out)


C1, C2, C3 = math.cos(math.pi / 8), math.cos(math.pi / 4), math.cos(3 * math.pi / 8)


def cosine_sums(first, s, last):
    p = [s[j - 1] + s[7 - j] for j in (1, 2, 3)]
    m = [s[j - 1] - s[7 - j] for j in (1, 2, 3)]
    mid = s[3]
    total, diff = first + last, first - last
    t = m[1] * C2
    u, v = diff + t, diff - t
    w1 = m[0] * C1 + m[2] * C3
    w3 = m[0] * C3 - m[2] * C1
    plus, minus = total + mid, total - mid
    outer, inner = p[0] + p[2], (p[0] - p[2]) * C2
    even = plus + p[1]
    return [
        even + outer, u + w1, minus + inner, v + w3, plus - p[1],
        v - w3, minus - inner, u - w1, even - outer,
    ]


def sine_sums(d):
    n = [d[j - 1] + d[7 - j] for j in (1, 2, 3)]
    r = [d[j - 1] - d[7 - j] for j in (1, 2, 3)]
    mid = d[3]
    y1 = n[0] * C3 + n[2] * C1
    y3 = n[0] * C1 - n[2] * C3
    g = n[1] * C2
    gp, gm = g + mid, g - mid
    e = (r[0] + r[2]) * C2
    return [y1 + gp, e + r[1], y3 + gm, r[0] - r[2], y3 - gm, e - r[1], y1 - gp]


def split_dot(x, weights):
    high = x.astype(jnp.bfloat16)
    low = (x - high.astype(jnp.float32)).astype(jnp.bfloat16)
    stacked = jnp.concatenate([high, low, high], axis=1)
    return jnp.dot(stacked, weights, preferred_element_type=jnp.float32)


def elastic_parts(strain, plastic, shear2):
    elastic = [strain[c] - plastic[c] for c in range(6)]
    volume = elastic[0] + elastic[1] + elastic[2]
    mean = volume * (1.0 / 3.0)
    dev = [elastic[c] - mean for c in range(3)] + elastic[3:]
    normal = dev[0] * dev[0] + dev[1] * dev[1] + dev[2] * dev[2]
    shear = dev[3] * dev[3] + dev[4] * dev[4] + dev[5] * dev[5]
    size = (normal + (shear + shear)) * (shear2 * shear2)
    return volume, dev, size


def solve(extent, rows, state, out, strain_cols, late_counts, mats, consts, scratch):
    bulk_ref, shear_ref, radius_ref = mats
    table_ref, plane_ref = consts
    pl_ref, e_ref, u_ref, a_ref, b_ref, a2_ref, b2_ref, t_ref = scratch
    half = extent // 2
    wide = extent * extent
    step = 6 * extent
    lanes = 128
    group = 6 * rows

    for c in range(6):
        column = jnp.broadcast_to(strain_cols[c], (rows, wide))
        for a in range(extent):
            for tile in range(wide // lanes):
                picked = state[tile, pl.ds(c * extent + a, rows, stride=step), :]
                pl_ref[c, a, :, pl.ds(tile * lanes, lanes)] = picked
            e_ref[c, a] = column
            u_ref[0, c, a] = jnp.zeros((rows, wide), jnp.float32)
            u_ref[1, c, a] = jnp.zeros((rows, wide), jnp.float32)
    count_col, top_count = late_counts()

    def current(a, tile, k, alpha, beta):
        lane = pl.ds(tile * lanes, lanes)
        newer, older = (k + 1) & 1, k & 1
        values = []
        for c in range(6):
            v = e_ref[c, a, :, lane] - alpha * u_ref[newer, c, a, :, lane]
            values.append(v - beta * u_ref[older, c, a, :, lane])
        plastic = [pl_ref[c, a, :, lane] for c in range(6)]
        shear2 = 2.0 * shear_ref[pl.ds(a, 1), lane]
        radius = radius_ref[pl.ds(a, 1), lane]
        bulk = bulk_ref[pl.ds(a, 1), lane]
        volume, dev, size = elastic_parts(values, plastic, shear2)
        factor = radius * lax.rsqrt(jnp.maximum(size, radius * radius))
        gain = factor * shear2
        pressure = bulk * volume
        stress = [gain * dev[c] + pressure for c in range(3)]
        stress += [gain * dev[c] for c in range(3, 6)]
        return values, plastic, dev, factor, stress

    def sweep(k, carry):
        alpha, beta, before = carry
        for a in range(extent):
            for tile in range(wide // lanes):
                lane = pl.ds(tile * lanes, lanes)
                values, _, _, _, stress = current(a, tile, k, alpha, beta)
                for c in range(6):
                    e_ref[c, a, :, lane] = values[c]
                    t_ref[c, a, :, lane] = stress[c]
        for c in range(6):
            for tile in range(wide // lanes):
                lane = pl.ds(tile * lanes, lanes)
                x = [t_ref[c, a, :, lane] for a in range(extent)]
                s = [x[j] + x[extent - j] for j in range(1, half)]
                d = [x[j] - x[extent - j] for j in range(1, half)]
                for kk, value in enumerate(cosine_sums(x[0], s, x[half])):
                    a_ref[pl.ds(kk * group + c * rows, rows), lane] = value
                for kk, value in enumerate(sine_sums(d)):
                    b_ref[pl.ds(kk * group + c * rows, rows), lane] = value
        a2_ref[...] = split_dot(a_ref[...], plane_ref[0])
        b2_ref[...] = split_dot(b_ref[...], plane_ref[1])
        for kk in range(half + 1):
            ends = kk == 0 or kk == half
            for tile in range(wide // lanes):
                lane = pl.ds(tile * lanes, lanes)
                coef = {}
                for index, pair in enumerate(SYM):
                    coef[pair] = table_ref[index, pl.ds(kk, 1), lane]
                    coef[pair[::-1]] = coef[pair]

                def place(c, odd):
                    if ends:
                        return a2_ref, a_ref, pl.ds(kk * group + c * rows, rows)
                    if (c >= 4) != odd:
                        return b2_ref, b_ref, pl.ds((kk - 1) * group + c * rows, rows)
                    return a2_ref, a_ref, pl.ds(kk * group + c * rows, rows)

                for odd in (False,) if ends else (False, True):
                    tau = []
                    for c in range(6):
                        src, _, where = place(c, odd)
                        value = src[where, lane]
                        tau.append(value if c < 3 else value + value)
                    for m in range(6):
                        acc = coef[m, 0] * tau[0]
                        for n in range(1, 6):
                            acc = acc + coef[m, n] * tau[n]
                        _, dst, where = place(m, odd)
                        dst[where, lane] = acc
        a2_ref[...] = split_dot(a_ref[...], plane_ref[0])
        b2_ref[...] = split_dot(b_ref[...], plane_ref[1])
        num = jnp.zeros((rows, lanes), jnp.float32)
        den = jnp.zeros((rows, lanes), jnp.float32)
        newest, last = k & 1, (k + 1) & 1
        for c in range(6):
            for tile in range(wide // lanes):
                lane = pl.ds(tile * lanes, lanes)
                ca = [a2_ref[pl.ds(kk * group + c * rows, rows), lane] for kk in range(half + 1)]
                sb = [b2_ref[pl.ds(kk * group + c * rows, rows), lane] for kk in range(half - 1)]
                even = cosine_sums(ca[0], ca[1:half], ca[half])
                odd = [None] + sine_sums(sb)
                for a in range(extent):
                    j = min(a, extent - a)
                    if a == 0 or a == half:
                        value = even[j]
                    elif a < half:
                        value = even[j] + odd[j]
                    else:
                        value = even[j] - odd[j]
                    change = value - u_ref[last, c, a, :, lane]
                    num = num + change * value
                    den = den + change * change
                    u_ref[newest, c, a, :, lane] = value
        scale = 1.0 / (6 * extent**3)
        top = jnp.sum(num, axis=1, keepdims=True) * scale
        bottom = jnp.sum(den, axis=1, keepdims=True) * scale + 1e-06
        weight = jnp.where(k > 0, top / bottom, 0.0)
        active = jnp.where(count_col > k.astype(jnp.float32), 1.0, 0.0)
        alpha = active * (1.0 - weight)
        beta = active * weight * before
        spread = lambda v: jnp.broadcast_to(v, (rows, lanes))
        return spread(alpha), spread(beta), weight

    zero = jnp.zeros((rows, lanes), jnp.float32)
    alpha, beta, _ = lax.fori_loop(
        0, top_count, sweep, (zero, zero, jnp.zeros((rows, 1), jnp.float32))
    )
    sums = [jnp.zeros((rows, lanes), jnp.float32) for _ in range(6)]
    for a in range(extent):
        for tile in range(wide // lanes):
            lane = pl.ds(tile * lanes, lanes)
            _, plastic, dev, factor, stress = current(a, tile, top_count, alpha, beta)
            rest = 1.0 - factor
            for c in range(6):
                sums[c] = sums[c] + stress[c]
                where = pl.ds(c * extent + a, rows, stride=step)
                out[tile, where, :] = plastic[c] + rest * dev[c]
    return sums


def solve_scratch(extent, rows):
    half, wide = extent // 2, extent * extent
    field = (6, extent, rows, wide)
    f32 = jnp.float32
    return [
        pltpu.VMEM(field, f32),
        pltpu.VMEM(field, f32),
        pltpu.VMEM((2,) + field, f32),
        pltpu.VMEM(((half + 1) * 6 * rows, wide), f32),
        pltpu.VMEM(((half - 1) * 6 * rows, wide), f32),
        pltpu.VMEM(((half + 1) * 6 * rows, wide), f32),
        pltpu.VMEM(((half - 1) * 6 * rows, wide), f32),
        pltpu.VMEM(field, f32),
    ]


def to_column(row, mask):
    return jnp.sum(jnp.where(mask, jnp.broadcast_to(row, mask.shape), 0.0), axis=1, keepdims=True)


def to_row(column, mask):
    return jnp.sum(jnp.where(mask, jnp.broadcast_to(column, mask.shape), 0.0), axis=0, keepdims=True)


def row_copies(hbm_row, stage, row, sems, extent):
    lanes = 128
    step = 6 * extent
    pairs = []
    for tile in range(extent * extent // lanes):
        inside = stage.at[tile, pl.ds(row * step, step), :]
        pairs.append((hbm_row.at[:, pl.ds(tile * lanes, lanes)], inside, sems.at[row, tile]))
    return pairs


def counts_column(counts, rows):
    where = lax.broadcasted_iota(jnp.int32, (rows, 1), 0)
    column = jnp.zeros((rows, 1), jnp.float32)
    top = counts[0]
    for r in range(rows):
        column = jnp.where(where == r, counts[r].astype(jnp.float32), column)
        top = jnp.maximum(top, counts[r])
    return column, top


def lane_mask(rows):
    shape = (rows, 128)
    return lax.broadcasted_iota(jnp.int32, shape, 0) == lax.broadcasted_iota(jnp.int32, shape, 1)


def spread_nodes(value):
    return value, pltpu.roll(value, 127, 1)


def strain_rows(corners):
    pairs = [spread_nodes(v) for v in corners]
    total = [lo + hi for lo, hi in pairs]
    rise = [hi - lo for lo, hi in pairs]
    h = [
        0.25 * ((total[1] + total[3]) - (total[0] + total[2])),
        0.25 * ((total[2] + total[3]) - (total[0] + total[1])),
        0.25 * ((rise[0] + rise[1]) + (rise[2] + rise[3])),
    ]
    pick = lambda i, j: h[j][i : i + 1]
    return [
        pick(0, 0), pick(1, 1), pick(2, 2),
        0.5 * (pick(1, 2) + pick(2, 1)),
        0.5 * (pick(0, 2) + pick(2, 0)),
        0.5 * (pick(0, 1) + pick(1, 0)),
    ]


def zero_below(value):
    return value, pltpu.roll(value, 1, 1)


def node_force(own, low_a, low_b, low_ab):
    total, rise = [], []
    for value in (own, low_a, low_b, low_ab):
        value, below = zero_below(value)
        total.append(value + below)
        rise.append(below - value)
    along = [
        (total[1] + total[3]) - (total[0] + total[2]),
        (total[2] + total[3]) - (total[0] + total[1]),
        (rise[0] + rise[1]) + (rise[2] + rise[3]),
    ]
    index = [[0, 5, 4], [5, 1, 3], [4, 3, 2]]
    rows = []
    for i in range(3):
        parts = [along[j][index[i][j] : index[i][j] + 1] for j in range(3)]
        rows.append(0.25 * (parts[0] + parts[1] + parts[2]))
    return rows


class Layout:
    def __init__(self, plastic_shape, depth, layers, columns):
        self.rows, _, self.extent, self.wide = plastic_shape
        self.depth, self.layers, self.columns = depth, layers, columns
        self.peers = min(layers // 2, self.rows // 2)
        self.capacity = self.rows // self.peers
        self.near = [k for k in (1, 2) if k < layers]
        self.early = (self.capacity * EARLY) // 4
        self.late = self.capacity - self.early
        self.step = 6 * self.extent
        self.meta = -(-self.capacity // 8) * 8

    def route(self, plan):
        here = lax.axis_index("rve")
        block = self.rows * self.columns
        partner = [lax.div(plan[e], block) for e in range(self.rows)]
        away = []
        for p in partner:
            d = p - here
            away.append(jnp.where(d < 0, d + self.layers, d))
        order = []
        for e in range(self.rows):
            before = jnp.int32(0)
            for f in range(e):
                before = before + (away[f] == away[e]).astype(jnp.int32)
            order.append(before)
        target = [lax.rem(plan[e], self.rows) for e in range(self.rows)]
        return away, order, target

    def pick(self, away, order, offset, place):
        row, found = jnp.int32(0), jnp.int32(0)
        for e in range(self.rows):
            hit = jnp.logical_and(away[e] == offset, order[e] == place)
            row = jnp.where(hit, e, row)
            found = jnp.where(hit, 1, found)
        return row, found


def pack_kernel(lay, *refs):
    displacement, plan, plastic = refs[:3]
    fixed = refs[3:8]
    nodes, state = refs[8:10]
    copied = refs[10:15]
    boxes = refs[15 : 15 + len(lay.near)]
    plan_s, corner, small_sems, box_sems, fix_sems, row_sems = refs[15 + len(lay.near) :]
    load_plan = pltpu.make_async_copy(plan, plan_s, small_sems.at[0])
    load_plan.start()
    load_corner = pltpu.make_async_copy(displacement, corner, small_sems.at[1])
    load_corner.start()
    copies = []
    for r in range(lay.rows):
        for src, dst, sem in row_copies(plastic.at[r], state, r, row_sems, lay.extent):
            copies.append(pltpu.make_async_copy(src, dst, sem))
    for i in range(len(fixed)):
        copies.append(pltpu.make_async_copy(fixed[i], copied[i], fix_sems.at[i]))
    for copy in copies:
        copy.start()
    nodes[...] = jnp.zeros(nodes.shape, jnp.float32)
    load_plan.wait()
    away, order, _ = lay.route(plan_s)
    packed = []
    for i, offset in enumerate(lay.near):
        for s in range(lay.early):
            row, _ = lay.pick(away, order, offset, s)
            packed.append(pltpu.make_async_copy(plastic.at[row], boxes[i].at[s], box_sems.at[i, s]))
            packed[-1].start()
    load_corner.wait()
    for i in range(3):
        nodes[i : i + 1, : lay.depth] = corner[i, 0]
    rare = jnp.int32(0)
    for e in range(lay.rows):
        usual = away[e] == 0
        for offset in lay.near:
            usual = jnp.logical_or(usual, away[e] == offset)
        rare = jnp.where(usual, rare, 1)
    nodes[3:4] = jnp.full((1, 128), rare.astype(jnp.float32))
    for copy in copies + packed:
        copy.wait()


def source_kernel(lay, *refs):
    extent, rows = lay.extent, lay.rows
    own, upper, side, counts, plan, state, bulk, shear, radius, table, plane = refs[:11]
    n = len(lay.near)
    finished, first = refs[11:13]
    others = refs[13 : 12 + n]
    at = 12 + max(n, 1)
    boxes = refs[at : at + n]
    counts_s, plan_s, small_sems, box_sems = refs[at + n : at + n + 4]
    scratch = refs[at + n + 4 :]
    small = [
        pltpu.make_async_copy(counts, counts_s, small_sems.at[0]),
        pltpu.make_async_copy(plan, plan_s, small_sems.at[1]),
    ]
    for copy in small:
        copy.start()
    mask = lane_mask(rows)
    inside = jnp.where(lax.axis_index("rve") < lay.layers - 1, 1.0, 0.0)
    corners = [own[0:3], upper[0:3] * inside, side[0:3], side[8:11] * inside]
    strain = [to_column(v, mask) for v in strain_rows(corners)]
    column = []

    def late_counts():
        for copy in small:
            copy.wait()
        values, top = counts_column(counts_s, rows)
        column.append(values)
        return values, top

    sums = solve(
        extent, rows, state, finished, strain, late_counts,
        (bulk, shear, radius), (table, plane), scratch,
    )
    away, order, target = lay.route(plan_s)
    stores = []
    for i, offset in enumerate(lay.near):
        for s in range(lay.late):
            row, _ = lay.pick(away, order, offset, lay.early + s)
            for tile in range(lay.wide // 128):
                start = pl.multiple_of(row * lay.step, 8)
                src = finished.at[tile, pl.ds(start, lay.step), :]
                dst = boxes[i].at[s, :, pl.ds(tile * 128, 128)]
                stores.append(pltpu.make_async_copy(src, dst, box_sems.at[i, s, tile]))
                stores[-1].start()
    lane = lax.broadcasted_iota(jnp.int32, (rows, 128), 1)
    sub = lax.broadcasted_iota(jnp.int32, (rows, 128), 0)
    card = jnp.zeros((rows, 128), jnp.float32)
    for c in range(6):
        card = jnp.where(lane == c, strain[c], card)
    card = jnp.where(lane == 6, column[0], card)
    for r in range(rows):
        label = (target[r] + 1).astype(jnp.float32)
        card = jnp.where(jnp.logical_and(lane == 7, sub == r), label, card)
    notes = (first,) + tuple(others)
    first[...] = jnp.zeros(first.shape, jnp.float32)
    for i, offset in enumerate(lay.near):
        base = 8 if i == 0 else 0
        if i:
            notes[i][...] = jnp.zeros(notes[i].shape, jnp.float32)
        for s in range(lay.capacity):
            row, found = lay.pick(away, order, offset, s)
            chosen = jnp.logical_and(sub == row, found > 0)
            line = jnp.sum(jnp.where(chosen, card, 0.0), axis=0, keepdims=True)
            line = jnp.where(lane[0:1] == 8, jnp.maximum(own[3:4], upper[3:4]), line)
            notes[i][base + s : base + s + 1] = line
    for c in range(6):
        mean = jnp.sum(sums[c], axis=1, keepdims=True) * (1.0 / extent**3)
        first[c : c + 1] = to_row(mean, mask)
    for copy in stores:
        copy.wait()


def note_row(i, s):
    return (8 if i == 0 else 0) + s


def target_kernel(lay, *refs):
    extent, rows, n = lay.extent, lay.rows, len(lay.near)
    notes, boxes = refs[:n], refs[n : 2 * n]
    own, upper, bulk, shear, radius, table, plane = refs[2 * n : 2 * n + 7]
    arrived, rare_out = refs[2 * n + 7 : 2 * n + 9]
    rest = refs[2 * n + 9 :]
    marks, rest = rest[:n], rest[n:]
    stage, result, load_sems, store_sems, mark_sems, cards = rest[:6]
    scratch = rest[6:]
    slots = [(i, s) for i in range(n) for s in range(lay.early)]
    reads = [pltpu.make_async_copy(notes[i], marks[i], mark_sems.at[i]) for i in range(n)]
    loads = []
    for r, (i, s) in enumerate(slots):
        for src, dst, sem in row_copies(boxes[i].at[s], stage, r, load_sems, extent):
            loads.append(pltpu.make_async_copy(src, dst, sem))
    for copy in reads + loads:
        copy.start()
    cards[...] = jnp.zeros(cards.shape, jnp.float32)
    for r, (i, s) in enumerate(slots):
        cards[r : r + 1] = notes[i][note_row(i, s) : note_row(i, s) + 1]
    card = cards[...]
    strain = [card[:, c : c + 1] for c in range(6)]

    def late_counts():
        for copy in reads:
            copy.wait()
        most = jnp.float32(0.0)
        for i, s in slots:
            most = jnp.maximum(most, marks[i][note_row(i, s), 6])
        return card[:, 6:7], most.astype(jnp.int32)

    rare = jnp.maximum(own[3:4], upper[3:4])
    for i in range(n):
        flag = notes[i][note_row(i, 0) : note_row(i, 0) + 1]
        rare = jnp.maximum(rare, jnp.broadcast_to(flag[:, 8:9], rare.shape))
    rare_out[...] = jnp.broadcast_to(rare, rare_out.shape)
    for copy in loads:
        copy.wait()
    solve(
        extent, rows, stage, result, strain, late_counts,
        (bulk, shear, radius), (table, plane), scratch,
    )
    moves = []
    for r, (i, s) in enumerate(slots):
        label = marks[i][note_row(i, s), 7].astype(jnp.int32)
        moves.append((r, label > 0, jnp.maximum(label - 1, 0)))
    for phase in ("start", "wait"):
        for r, valid, where in moves:

            @pl.when(valid)
            def _(r=r, where=where, phase=phase):
                for dst, src, sem in row_copies(arrived.at[where], result, r, store_sems, extent):
                    getattr(pltpu.make_async_copy(src, dst, sem), phase)()


def place_kernel(lay, *refs):
    n = len(lay.near)
    notes, boxes = refs[:n], refs[n : 2 * n]
    plan, finished, _, out = refs[2 * n : 2 * n + 4]
    marks, rest = refs[2 * n + 4 : 3 * n + 4], refs[3 * n + 4 :]
    plan_s, mark_sems, box_sems, row_sems = rest
    reads = [pltpu.make_async_copy(notes[i], marks[i], mark_sems.at[i]) for i in range(n)]
    reads.append(pltpu.make_async_copy(plan, plan_s, mark_sems.at[n]))
    for copy in reads:
        copy.start()
    for copy in reads:
        copy.wait()
    away, _, target = lay.route(plan_s)
    moves = []
    for i in range(n):
        for s in range(lay.late):
            label = marks[i][note_row(i, lay.early + s), 7].astype(jnp.int32)
            where = jnp.maximum(label - 1, 0)
            moves.append((label > 0, [(boxes[i].at[s], out.at[where], box_sems.at[i, s])]))
    for e in range(lay.rows):
        pieces = row_copies(out.at[target[e]], finished, e, row_sems, lay.extent)
        moves.append((away[e] == 0, [(src, dst, sem) for dst, src, sem in pieces]))
    for phase in ("start", "wait"):
        for valid, pieces in moves:

            @pl.when(valid)
            def _(pieces=pieces, phase=phase):
                for src, dst, sem in pieces:
                    getattr(pltpu.make_async_copy(src, dst, sem), phase)()


def force_kernel(lay, own, below, side, out):
    inside = jnp.where(lax.axis_index("rve") > 0, 1.0, 0.0)
    rows = node_force(own[0:6], below[0:6] * inside, side[0:6], side[8:14] * inside)
    for i in range(3):
        out[i, 0] = rows[i][:, : lay.depth]


def shift_pairs(counts, steps):
    pairs = []
    for flat in range(math.prod(counts)):
        at, rest = [], flat
        for size in reversed(counts):
            at.insert(0, rest % size)
            rest //= size
        to = [p + s for p, s in zip(at, steps)]
        if all(0 <= t < size for t, size in zip(to, counts)):
            target = 0
            for t, size in zip(to, counts):
                target = target * size + t
            pairs.append((flat, target))
    return pairs


def ring(value, step):
    layers = lax.axis_size("rve")
    return lax.ppermute(value, "rve", [(i, (i + step) % layers) for i in range(layers)])


def sideways(value, step):
    columns = lax.axis_size("mic") * lax.axis_size("mac")
    return lax.ppermute(value, ("mic", "mac"), shift_pairs([columns], [step]))


def route_slots(migration_plan, width_rows, capacity):
    columns = lax.axis_size("mic") * lax.axis_size("mac")
    partner = migration_plan // width_rows // columns
    target_row = migration_plan % width_rows
    shared = partner[:, None] == partner[None, :]
    positions = jnp.arange(width_rows)
    earlier = positions[:, None] > positions[None, :]
    order_within = jnp.sum((shared & earlier).astype(jnp.int32), axis=1)
    return (partner * capacity + order_within, target_row)


def move_any(rows_next, migration_plan):
    width_rows = rows_next.shape[0]
    devices_along = lax.axis_size("rve")
    peers_used = min(devices_along // 2, width_rows // 2)
    capacity = width_rows // peers_used
    total = devices_along * capacity
    slot_index, target_row = route_slots(migration_plan, width_rows, capacity)
    matches = slot_index[None, :] == jnp.arange(total)[:, None]
    source = jnp.sum(jnp.where(matches, jnp.arange(width_rows)[None, :], 0), axis=1)
    labels = jnp.sum(jnp.where(matches, target_row[None, :] + 1, 0), axis=1)
    outgoing = jnp.take(rows_next, source, axis=0)
    arrived = lax.all_to_all(outgoing, "rve", split_axis=0, concat_axis=0, tiled=True)
    tags = lax.all_to_all(labels, "rve", split_axis=0, concat_axis=0, tiled=True)
    wanted = tags[None, :] == jnp.arange(1, width_rows + 1)[:, None]
    place = jnp.sum(jnp.where(wanted, jnp.arange(total)[None, :], 0), axis=1)
    return jnp.take(arrived, place, axis=0)


def in_hbm(value):
    return pltpu.with_memory_space_constraint(value, pltpu.HBM)


def in_vmem(value):
    return pltpu.with_memory_space_constraint(value, pltpu.VMEM)


def on_device(displacement, plastic, bulk, shear, radius, counts, migration_plan):
    layers = lax.axis_size("rve")
    columns = lax.axis_size("mic") * lax.axis_size("mac")
    lay = Layout(plastic.shape, displacement.shape[3], layers, columns)
    fast = layers <= 2 + len(lay.near)
    if not fast:
        lay.near = []
    rows, extent, wide, n = lay.rows, lay.extent, lay.wide, len(lay.near)
    f32 = jnp.float32
    tiles = wide // 128
    fixed = [bulk, shear, radius, jnp.asarray(symbol_table(extent)), jnp.asarray(plane_tables(extent))]
    vmem = pl.BlockSpec(memory_space=pltpu.VMEM)
    anywhere = pl.BlockSpec(memory_space=pl.ANY)
    sem = pltpu.SemaphoreType.DMA
    params = pltpu.CompilerParams(vmem_limit_bytes=VMEM_BYTES)
    staging = pltpu.VMEM((tiles, rows * lay.step, 128), f32)
    small = pltpu.SMEM((rows,), jnp.int32)
    plan = in_hbm(migration_plan)
    nodes, state, *rest = pl.pallas_call(
        lambda *refs: pack_kernel(lay, *refs),
        out_shape=[pltpu.VMEM((8, 128), f32), staging]
        + [pltpu.VMEM(v.shape, v.dtype) for v in fixed]
        + [pltpu.VMEM((lay.early, lay.step, wide), f32)] * n,
        in_specs=[anywhere] * 8,
        out_specs=[vmem] * (7 + n),
        scratch_shapes=[
            small,
            pltpu.VMEM(displacement.shape, f32),
            sem((2,)),
            sem((max(n, 1), max(lay.early, 1))),
            sem((5,)),
            sem((rows, tiles)),
        ],
        name="pack",
    )(in_hbm(displacement), plan, in_hbm(plastic.reshape(rows, lay.step, wide)), *[in_hbm(v) for v in fixed])
    fixed = [in_vmem(v) for v in rest[:5]]
    raw = rest[5:]
    upper = ring(nodes, -1)
    for i, offset in enumerate(lay.near):
        raw[i] = ring(raw[i], offset)
    both = jnp.concatenate([nodes, upper], axis=0)
    side = sideways(both, -1)
    nodes, upper = in_vmem(nodes), in_vmem(upper)
    outs = [staging, pltpu.VMEM((8 + lay.meta, 128), f32)]
    outs += [pltpu.VMEM((lay.meta, 128), f32)] * (n - 1)
    outs += [pltpu.VMEM((lay.late, lay.step, wide), f32)] * n
    finished, *rest = pl.pallas_call(
        lambda *refs: source_kernel(lay, *refs),
        out_shape=outs,
        in_specs=[vmem] * 3 + [anywhere] * 2 + [vmem] * 6,
        out_specs=[vmem] * len(outs),
        scratch_shapes=[small, small, sem((2,)), sem((max(n, 1), max(lay.late, 1), tiles))]
        + solve_scratch(extent, rows),
        compiler_params=params,
        name="solve_source",
    )(nodes, upper, in_vmem(side), in_hbm(counts), plan, in_vmem(state), *fixed)
    first, others, done = rest[0], rest[1:n], rest[max(n, 1) :]
    below = ring(first, 1)
    notes = [below]
    for i, offset in enumerate(lay.near[1:]):
        notes.append(ring(others[i], offset))
    for i, offset in enumerate(lay.near):
        done[i] = ring(done[i], offset)
    pair = jnp.concatenate([first[:8], below[:8]], axis=0)
    beside = sideways(pair, 1)
    force = pl.pallas_call(
        lambda *refs: force_kernel(lay, *refs),
        out_shape=jax.ShapeDtypeStruct(displacement.shape, f32),
        in_specs=[vmem] * 3,
        out_specs=vmem,
        name="force",
    )(in_vmem(first), in_vmem(below), in_vmem(beside))

    def unusual(_):
        rows_first = finished.reshape(tiles, rows, lay.step, 128).transpose(1, 2, 0, 3)
        return move_any(rows_first.reshape(rows, lay.step, wide), migration_plan)

    if not fast:
        return force, unusual(None).reshape(plastic.shape)
    notes = [in_vmem(v) for v in notes]
    marks = [pltpu.SMEM(v.shape, f32) for v in notes]
    arrived, rare = pl.pallas_call(
        lambda *refs: target_kernel(lay, *refs),
        out_shape=[pltpu.HBM((rows, lay.step, wide), f32), jax.ShapeDtypeStruct((8, 128), f32)],
        in_specs=[vmem] * n + [vmem] * n + [vmem] * 7,
        out_specs=[anywhere, vmem],
        scratch_shapes=marks
        + [staging, staging, sem((rows, tiles)), sem((rows, tiles)), sem((n,))]
        + [pltpu.VMEM((rows, 128), f32)]
        + solve_scratch(extent, rows),
        compiler_params=params,
        name="solve_target",
    )(*notes, *[in_vmem(v) for v in raw], nodes, upper, *fixed)
    moved = pl.pallas_call(
        lambda *refs: place_kernel(lay, *refs),
        out_shape=pltpu.HBM((rows, lay.step, wide), f32),
        in_specs=[vmem] * (2 * n) + [anywhere, vmem, anywhere],
        out_specs=anywhere,
        scratch_shapes=marks
        + [small, sem((n + 1,)), sem((n, lay.late)), sem((rows, tiles))],
        input_output_aliases={2 * n + 2: 0},
        compiler_params=params,
        name="place",
    )(*notes, *[in_vmem(v) for v in done], plan, in_vmem(finished), in_hbm(arrived))
    moved = lax.cond(rare[0, 0] > 0.0, unusual, lambda v: v, moved)
    return force, moved.reshape(plastic.shape)


def solution(mesh):
    everyone = ("rve", "mic", "mac")

    return jax.shard_map(
        on_device,
        mesh=mesh,
        in_specs=(
            P(None, "rve", ("mic", "mac"), None),
            P(everyone, None, None, None),
            P(), P(), P(),
            P(everyone),
            P(everyone),
        ),
        out_specs=(P(None, "rve", ("mic", "mac"), None), P(everyone, None, None, None)),
        check_vma=False,
    )
```

profile of v0, /device:TPU:20, one launch (start us, length us, event | category | flops | bytes accessed | tf_op | source)
XLA Modules:
  0.0 60.1 jit_solution(6614277453648361864)
XLA Ops:
  0.6 3.0 %pack.1 = (f32[8,128]{1,0:T(8,128)S(1)}, f32[2,768,128]{2,1,0:T(8,128)S(1)}, f32[16,256]{1,0:T(8,128)S(1)}, f32[16,256]{1,0:T(8,128)S(1)}, f32[16,256]{1,0:T(8,1...) custom-call(f32[3,1,1,8]{3,2,1,0:T(1,128)} %refs_0_.1, ...), custom_call_target="tpu_custom_call" | custom-call | tf_op jit(solution)/shard_map/pack/pallas_call | solution.py:677
  3.6 0.5 collective-permute-start
  4.1 3.2 %collective-permute-done.refs_1_.refs_5_ = f32[8,128]{1,0:T(8,128)S(1)} collective-permute-done((f32[8,128]{1,0:T(8,128)S(1)}, f32[8,128]{1,0:T(8,128)S(1)}, u32[]{:S(2)}, u32[]{:S(2)}) %collective-permute-start) | collective-permute-done | bytes 4128 | tf_op jit(solution)/shard_map/ppermute | solution.py:614
  7.3 1.9 %collective-permute-start.1 = (f32[16,128]{1,0:T(8,128)S(1)}, f32[16,128]{1,0:T(8,128)S(1)}, u32[]{:S(2)}, u32[]{:S(2)}) collective-permute-start(f32[16,128]{1,0:T(8,128)S(1)} %pad_maximum_fusion), channel_id=1, source_target_pairs={{1,0},{2,1},{3,2},{4,3},{5,4},{6,5},{7,6},{9,8},{10,9},{11,10},{12... | collective-permute-start | bytes 24584 | tf_op jit(solution)/shard_map/ppermute | solution.py:619
  9.2 3.4 %collective-permute-start.5 = (f32[2,96,256]{2,1,0:T(8,128)}, f32[2,96,256]{2,1,0:T(8,128)S(1)}, u32[]{:S(2)}, u32[]{:S(2)}) collective-permute-start(f32[2,96,256]{2,1,0:T(8,128)} %get-tuple-element.39), channel_id=1, source_target_pairs={{0,8},{8,16},{16,24},{24,0},{1,9},{9,17},{17,25},{25,1},{2,10},{10... | collective-permute-start | bytes 589832 | tf_op jit(solution)/shard_map/ppermute | solution.py:614
  12.6 0.0 collective-permute-start.6
  12.6 0.0 collective-permute-done.1.refs_2_
  12.6 4.5 %solve_source.1 = (f32[2,768,128]{2,1,0:T(8,128)S(1)}, f32[16,128]{1,0:T(8,128)S(1)}, f32[8,128]{1,0:T(8,128)S(1)}, f32[2,96,256]{2,1,0:T(8,128)}, f32[2,96,256]{2,1,0:T(8,128)}) custom-call(f32[8,128]{1,0:T(8,128)S(1)} %get-tuple-element.30.refs_0_.refs_4_, f32[8,128]{1,0:T(8,128)S(1)} %collective-permute-done.refs_1_.refs_5_, ...), custom_call_target="tpu_custom_call" | custom-call | tf_op jit(solution)/shard_map/solve_source/pallas_call | solution.py:705
  17.2 1.3 %collective-permute-start.7 = (f32[2,96,256]{2,1,0:T(8,128)}, f32[2,96,256]{2,1,0:T(8,128)S(1)}, u32[]{:S(2)}, u32[]{:S(2)}) collective-permute-start(f32[2,96,256]{2,1,0:T(8,128)} %get-tuple-element.42), channel_id=1, source_target_pairs={{0,8},{8,16},{16,24},{24,0},{1,9},{9,17},{17,25},{25,1},{2,10},{10... | collective-permute-start | bytes 589832 | tf_op jit(solution)/shard_map/ppermute | solution.py:614
  18.5 5.6 %collective-permute-start.8 = (f32[2,96,256]{2,1,0:T(8,128)}, f32[2,96,256]{2,1,0:T(8,128)S(1)}, u32[]{:S(2)}, u32[]{:S(2)}) collective-permute-start(f32[2,96,256]{2,1,0:T(8,128)} %get-tuple-element.43), channel_id=1, source_target_pairs={{0,16},{8,24},{16,0},{24,8},{1,17},{9,25},{17,1},{25,9},{2,18},{10... | collective-permute-start | bytes 589832 | tf_op jit(solution)/shard_map/ppermute | solution.py:614
  24.1 1.4 %collective-permute-start.2 = (f32[16,128]{1,0:T(8,128)S(1)}, f32[16,128]{1,0:T(8,128)S(1)}, u32[]{:S(2)}, u32[]{:S(2)}) collective-permute-start(f32[16,128]{1,0:T(8,128)S(1)} %get-tuple-element.37.refs_0_), channel_id=1, source_target_pairs={{0,8},{8,16},{16,24},{24,0},{1,9},{9,17},{17,25},{25,1},{2,10},{10... | collective-permute-start | bytes 24584 | tf_op jit(solution)/shard_map/ppermute | solution.py:614
  25.5 12.6 %collective-permute-done.2.refs_1_.refs_0_ = f32[16,128]{1,0:T(8,128)S(1)} collective-permute-done((f32[16,128]{1,0:T(8,128)S(1)}, f32[16,128]{1,0:T(8,128)S(1)}, u32[]{:S(2)}, u32[]{:S(2)}) %collective-permute-start.2) | collective-permute-done | bytes 8224 | tf_op jit(solution)/shard_map/ppermute | solution.py:614
  38.1 1.9 %collective-permute-start.3 = (f32[16,128]{1,0:T(8,128)S(1)}, f32[16,128]{1,0:T(8,128)S(1)}, u32[]{:S(2)}, u32[]{:S(2)}) collective-permute-start(f32[16,128]{1,0:T(8,128)S(1)} %pad_maximum_fusion.1), channel_id=1, source_target_pairs={{0,1},{1,2},{2,3},{3,4},{4,5},{5,6},{6,7},{8,9},{9,10},{10,11},{11... | collective-permute-start | bytes 24584 | tf_op jit(solution)/shard_map/ppermute | solution.py:619
  40.0 3.9 %collective-permute-done.3.refs_2_ = f32[16,128]{1,0:T(8,128)S(1)} collective-permute-done((f32[16,128]{1,0:T(8,128)S(1)}, f32[16,128]{1,0:T(8,128)S(1)}, u32[]{:S(2)}, u32[]{:S(2)}) %collective-permute-start.3) | collective-permute-done | bytes 8224 | tf_op jit(solution)/shard_map/ppermute | solution.py:619
  44.0 0.0 collective-permute-start.4
  44.0 0.6 %force.1 = f32[3,1,1,8]{3,2,1,0:T(1,128)} custom-call(f32[16,128]{1,0:T(8,128)S(1)} %get-tuple-element.37.refs_0_, f32[16,128]{1,0:T(8,128)S(1)} %collective-permute-done.2.refs_1_.refs_0_, f32[16,128]{1,0:T(8,128)S(1)} %collective-permute-done.3.refs_2_), custom_call_target="tpu_custom_call" | custom-call | tf_op jit(solution)/shard_map/force/pallas_call | solution.py:724
  44.6 3.9 %collective-permute-done.4.refs_1_ = f32[8,128]{1,0:T(8,128)S(1)} collective-permute-done((f32[8,128]{1,0:T(8,128)S(1)}, f32[8,128]{1,0:T(8,128)S(1)}, u32[]{:S(2)}, u32[]{:S(2)}) %collective-permute-start.4) | collective-permute-done | bytes 4128 | tf_op jit(solution)/shard_map/ppermute | solution.py:614
  48.5 0.0 collective-permute-done.5.refs_2_
  48.5 0.0 collective-permute-done.6.refs_3_
  48.5 8.6 %solve_target.1 = (f32[8,96,256]{2,1,0:T(8,128)}, f32[8,128]{1,0:T(8,128)S(1)}) custom-call(f32[16,128]{1,0:T(8,128)S(1)} %collective-permute-done.2.refs_1_.refs_0_, f32[8,128]{1,0:T(8,128)S(1)} %collective-permute-done.4.refs_1_, f32[2,96,256]{2,1,0:T(8,128)S(1)} %collective-permute-done.5.refs_2_, f32[2,96,256]{2,1,0:T(8,128)S(1)} %collective-permute-done.6.refs_3_, ...), custom_call_target="tpu_custom_call" | custom-call | tf_op jit(solution)/shard_map/solve_target/pallas_call | solution.py:740
  57.1 0.0 copy-start
  57.1 0.5 slice.11
  58.2 0.0 collective-permute-done.7.refs_2_
  58.3 0.0 collective-permute-done.8.refs_3_
  58.3 1.8 %place.1 = f32[8,96,256]{2,1,0:T(8,128)} custom-call(f32[16,128]{1,0:T(8,128)S(1)} %collective-permute-done.2.refs_1_.refs_0_, f32[8,128]{1,0:T(8,128)S(1)} %collective-permute-done.4.refs_1_, f32[2,96,256]{2,1,0:T(8,128)S(1)} %collective-permute-done.7.refs_2_, f32[2,96,256]{2,1,0:T(8,128)S(1)} %collective-permute-done.8.refs_3_, ...), custom_call_target="tpu_custom_call", output_to_operand_aliasing={{}: (6, {})} | custom-call | tf_op jit(solution)/shard_map/place/pallas_call | solution.py:752
  60.1 0.0 copy-done
  (5 shorter events, 0.0 us)
Async XLA Ops:
  3.6 3.7 %collective-permute-start = (f32[8,128]{1,0:T(8,128)S(1)}, f32[8,128]{1,0:T(8,128)S(1)}, u32[]{:S(2)}, u32[]{:S(2)}) collective-permute-start(f32[8,128]{1,0:T(8,128)S(1)} %get-tuple-element.30.refs_0_.refs_4_), channel_id=1, source_target_pairs={{0,24},{8,0},{16,8},{24,16},{1,25},{9,1},{17,9},{25,17},{2,26},{10... | collective-permute-start | bytes 12296 | tf_op jit(solution)/shard_map/ppermute | solution.py:614
  7.3 5.3 %collective-permute-start.1 = (f32[16,128]{1,0:T(8,128)S(1)}, f32[16,128]{1,0:T(8,128)S(1)}, u32[]{:S(2)}, u32[]{:S(2)}) collective-permute-start(f32[16,128]{1,0:T(8,128)S(1)} %pad_maximum_fusion), channel_id=1, source_target_pairs={{1,0},{2,1},{3,2},{4,3},{5,4},{6,5},{7,6},{9,8},{10,9},{11,10},{12... | collective-permute-start | bytes 24584 | tf_op jit(solution)/shard_map/ppermute | solution.py:619
  9.2 39.3 %collective-permute-start.5 = (f32[2,96,256]{2,1,0:T(8,128)}, f32[2,96,256]{2,1,0:T(8,128)S(1)}, u32[]{:S(2)}, u32[]{:S(2)}) collective-permute-start(f32[2,96,256]{2,1,0:T(8,128)} %get-tuple-element.39), channel_id=1, source_target_pairs={{0,8},{8,16},{16,24},{24,0},{1,9},{9,17},{17,25},{25,1},{2,10},{10... | collective-permute-start | bytes 589832 | tf_op jit(solution)/shard_map/ppermute | solution.py:614
  12.6 35.8 %collective-permute-start.6 = (f32[2,96,256]{2,1,0:T(8,128)}, f32[2,96,256]{2,1,0:T(8,128)S(1)}, u32[]{:S(2)}, u32[]{:S(2)}) collective-permute-start(f32[2,96,256]{2,1,0:T(8,128)} %get-tuple-element.40), channel_id=1, source_target_pairs={{0,16},{8,24},{16,0},{24,8},{1,17},{9,25},{17,1},{25,9},{2,18},{10... | collective-permute-start | bytes 589832 | tf_op jit(solution)/shard_map/ppermute | solution.py:614
  17.2 41.1 %collective-permute-start.7 = (f32[2,96,256]{2,1,0:T(8,128)}, f32[2,96,256]{2,1,0:T(8,128)S(1)}, u32[]{:S(2)}, u32[]{:S(2)}) collective-permute-start(f32[2,96,256]{2,1,0:T(8,128)} %get-tuple-element.42), channel_id=1, source_target_pairs={{0,8},{8,16},{16,24},{24,0},{1,9},{9,17},{17,25},{25,1},{2,10},{10... | collective-permute-start | bytes 589832 | tf_op jit(solution)/shard_map/ppermute | solution.py:614
  18.5 39.7 %collective-permute-start.8 = (f32[2,96,256]{2,1,0:T(8,128)}, f32[2,96,256]{2,1,0:T(8,128)S(1)}, u32[]{:S(2)}, u32[]{:S(2)}) collective-permute-start(f32[2,96,256]{2,1,0:T(8,128)} %get-tuple-element.43), channel_id=1, source_target_pairs={{0,16},{8,24},{16,0},{24,8},{1,17},{9,25},{17,1},{25,9},{2,18},{10... | collective-permute-start | bytes 589832 | tf_op jit(solution)/shard_map/ppermute | solution.py:614
  24.1 14.0 %collective-permute-start.2 = (f32[16,128]{1,0:T(8,128)S(1)}, f32[16,128]{1,0:T(8,128)S(1)}, u32[]{:S(2)}, u32[]{:S(2)}) collective-permute-start(f32[16,128]{1,0:T(8,128)S(1)} %get-tuple-element.37.refs_0_), channel_id=1, source_target_pairs={{0,8},{8,16},{16,24},{24,0},{1,9},{9,17},{17,25},{25,1},{2,10},{10... | collective-permute-start | bytes 24584 | tf_op jit(solution)/shard_map/ppermute | solution.py:614
  38.1 5.9 %collective-permute-start.3 = (f32[16,128]{1,0:T(8,128)S(1)}, f32[16,128]{1,0:T(8,128)S(1)}, u32[]{:S(2)}, u32[]{:S(2)}) collective-permute-start(f32[16,128]{1,0:T(8,128)S(1)} %pad_maximum_fusion.1), channel_id=1, source_target_pairs={{0,1},{1,2},{2,3},{3,4},{4,5},{5,6},{6,7},{8,9},{9,10},{10,11},{11... | collective-permute-start | bytes 24584 | tf_op jit(solution)/shard_map/ppermute | solution.py:619
  44.0 4.5 %collective-permute-start.4 = (f32[8,128]{1,0:T(8,128)S(1)}, f32[8,128]{1,0:T(8,128)S(1)}, u32[]{:S(2)}, u32[]{:S(2)}) collective-permute-start(f32[8,128]{1,0:T(8,128)S(1)} %get-tuple-element.38), channel_id=1, source_target_pairs={{0,16},{8,24},{16,0},{24,8},{1,17},{9,25},{17,1},{25,9},{2,18},{10... | collective-permute-start | bytes 12296 | tf_op jit(solution)/shard_map/ppermute | solution.py:614
  57.1 3.0 %copy-start = (s32[8]{0:T(128)S(1)}, s32[8]{0:T(128)}, u32[]{:S(2)}) copy-start(s32[8]{0:T(128)} %refs_4_.5) | copy-start | bytes 100
where the time goes:
time: 60.3 us; the launch traced here: 60.1 us
  waiting for transfers between devices  23.6 us (39%)
  Pallas kernels  18.6 us (31%)
  starting transfers between devices  16.1 us (27%)
  between operations  1.34 us (2%)
    ppermute x7, waiting for transfers between devices, ring(): lax.ppermute(value, 'rve', [(i, (i + step) % layers) for i in range(layer...  19.6 us
    ppermute x7, starting transfers between devices, ring(): lax.ppermute(value, 'rve', [(i, (i + step) % layers) for i in range(layer...  12.2 us
    pallas_call x1, Pallas kernels, on_device(): pl.pallas_call(lambda *refs: target_kernel(lay, *refs), out_shape=[pltpu....  8.58 us
    pallas_call x1, Pallas kernels, on_device(): pl.pallas_call(lambda *refs: source_kernel(lay, *refs), out_shape=outs, i...  4.54 us
    ppermute x2, waiting for transfers between devices, sideways(): return lax.ppermute(value, ('mic', 'mac'), shift_pairs([columns], [step]))  3.94 us
    ppermute x2, starting transfers between devices, sideways(): return lax.ppermute(value, ('mic', 'mac'), shift_pairs([columns], [step]))  3.82 us
    pallas_call x1, Pallas kernels, on_device(): pl.pallas_call(lambda *refs: pack_kernel(lay, *refs), out_shape=[pltpu.VM...  2.99 us
    pallas_call x1, Pallas kernels, on_device(): pl.pallas_call(lambda *refs: place_kernel(lay, *refs), out_shape=pltpu.HB...  1.82 us
  transfers between devices with their start and end apart: 9, of which 4 were waited for; matrix products, arithmetic and copies ran while one was open for 1% of the time, Pallas kernels for 23%

commit v1 on v0

--- a/solution.py
+++ b/solution.py
@@ -11,7 +11,7 @@
 
 COUPLING = 0.7
 EARLY = 2
-VMEM_BYTES = 48 * 2**20
+VMEM_BYTES = 20 * 2**20
 PAIRS = [(0, 0), (1, 1), (2, 2), (1, 2), (0, 2), (0, 1)]
 SYM = [(m, n) for m in range(6) for n in range(m, 6)]
 
@@ -110,22 +110,18 @@
     return volume, dev, size
 
 
-def solve(extent, rows, state, out, strain_cols, late_counts, mats, consts, scratch):
-    bulk_ref, shear_ref, radius_ref = mats
+def solve(extent, rows, state, out, strain_cols, late_counts, consts, scratch, ship=None):
     table_ref, plane_ref = consts
-    pl_ref, e_ref, u_ref, a_ref, b_ref, a2_ref, b2_ref, t_ref = scratch
+    bulk_ref, shear_ref, radius_ref = [table_ref.at[len(SYM) + i] for i in range(3)]
+    e_ref, u_ref, a_ref, b_ref, a2_ref, b2_ref, t_ref = scratch
     half = extent // 2
     wide = extent * extent
-    step = 6 * extent
     lanes = 128
     group = 6 * rows
 
     for c in range(6):
         column = jnp.broadcast_to(strain_cols[c], (rows, wide))
         for a in range(extent):
-            for tile in range(wide // lanes):
-                picked = state[tile, pl.ds(c * extent + a, rows, stride=step), :]
-                pl_ref[c, a, :, pl.ds(tile * lanes, lanes)] = picked
             e_ref[c, a] = column
             u_ref[0, c, a] = jnp.zeros((rows, wide), jnp.float32)
             u_ref[1, c, a] = jnp.zeros((rows, wide), jnp.float32)
@@ -138,7 +134,7 @@
         for c in range(6):
             v = e_ref[c, a, :, lane] - alpha * u_ref[newer, c, a, :, lane]
             values.append(v - beta * u_ref[older, c, a, :, lane])
-        plastic = [pl_ref[c, a, :, lane] for c in range(6)]
+        plastic = [state[c, a, :, lane] for c in range(6)]
         shear2 = 2.0 * shear_ref[pl.ds(a, 1), lane]
         radius = radius_ref[pl.ds(a, 1), lane]
         bulk = bulk_ref[pl.ds(a, 1), lane]
@@ -245,8 +241,9 @@
             rest = 1.0 - factor
             for c in range(6):
                 sums[c] = sums[c] + stress[c]
-                where = pl.ds(c * extent + a, rows, stride=step)
-                out[tile, where, :] = plastic[c] + rest * dev[c]
+                out[c, a, :, lane] = plastic[c] + rest * dev[c]
+        if ship and a % half == half - 1:
+            ship(a // half)
     return sums
 
 
@@ -255,7 +252,6 @@
     field = (6, extent, rows, wide)
     f32 = jnp.float32
     return [
-        pltpu.VMEM(field, f32),
         pltpu.VMEM(field, f32),
         pltpu.VMEM((2,) + field, f32),
         pltpu.VMEM(((half + 1) * 6 * rows, wide), f32),
@@ -272,16 +268,6 @@
 
 def to_row(column, mask):
     return jnp.sum(jnp.where(mask, jnp.broadcast_to(column, mask.shape), 0.0), axis=0, keepdims=True)
-
-
-def row_copies(hbm_row, stage, row, sems, extent):
-    lanes = 128
-    step = 6 * extent
-    pairs = []
-    for tile in range(extent * extent // lanes):
-        inside = stage.at[tile, pl.ds(row * step, step), :]
-        pairs.append((hbm_row.at[:, pl.ds(tile * lanes, lanes)], inside, sems.at[row, tile]))
-    return pairs
 
 
 def counts_column(counts, rows):
@@ -353,7 +339,8 @@
         self.near = [k for k in (1, 2) if k < layers]
         self.early = (self.capacity * EARLY) // 4
         self.late = self.capacity - self.early
-        self.step = 6 * self.extent
+        self.row = (6, self.extent, self.wide)
+        self.field = (6, self.extent, self.rows, self.wide)
         self.meta = -(-self.capacity // 8) * 8
 
     def route(self, plan):
@@ -373,6 +360,10 @@
         target = [lax.rem(plan[e], self.rows) for e in range(self.rows)]
         return away, order, target
 
+    def late_slots(self):
+        places = range(self.early, self.capacity)
+        return [(i, s) for i in range(len(self.near)) for s in places]
+
     def pick(self, away, order, offset, place):
         row, found = jnp.int32(0), jnp.int32(0)
         for e in range(self.rows):
@@ -383,24 +374,20 @@
 
 
 def pack_kernel(lay, *refs):
-    displacement, plan, plastic = refs[:3]
-    fixed = refs[3:8]
-    nodes, state = refs[8:10]
-    copied = refs[10:15]
+    displacement, plan, counts, plastic = refs[:4]
+    plane, table, *fields = refs[4:9]
+    nodes, state, plane_copy, board, plan_s, counts_s = refs[9:15]
     boxes = refs[15 : 15 + len(lay.near)]
-    plan_s, corner, small_sems, box_sems, fix_sems, row_sems = refs[15 + len(lay.near) :]
+    corner, small_sems, box_sems, fix_sems, row_sems = refs[15 + len(lay.near) :]
     load_plan = pltpu.make_async_copy(plan, plan_s, small_sems.at[0])
     load_plan.start()
     load_corner = pltpu.make_async_copy(displacement, corner, small_sems.at[1])
     load_corner.start()
-    copies = []
+    copies = [pltpu.make_async_copy(counts, counts_s, small_sems.at[2])]
+    copies[0].start()
     for r in range(lay.rows):
-        for src, dst, sem in row_copies(plastic.at[r], state, r, row_sems, lay.extent):
-            copies.append(pltpu.make_async_copy(src, dst, sem))
-    for i in range(len(fixed)):
-        copies.append(pltpu.make_async_copy(fixed[i], copied[i], fix_sems.at[i]))
-    for copy in copies:
-        copy.start()
+        copies.append(pltpu.make_async_copy(plastic.at[r], state.at[:, :, r, :], row_sems.at[r]))
+        copies[-1].start()
     nodes[...] = jnp.zeros(nodes.shape, jnp.float32)
     load_plan.wait()
     away, order, _ = lay.route(plan_s)
@@ -410,6 +397,11 @@
             row, _ = lay.pick(away, order, offset, s)
             packed.append(pltpu.make_async_copy(plastic.at[row], boxes[i].at[s], box_sems.at[i, s]))
             packed[-1].start()
+    fixed = [(plane, plane_copy), (table, board.at[pl.ds(0, len(SYM))])]
+    fixed += [(field, board.at[len(SYM) + i]) for i, field in enumerate(fields)]
+    for i, (src, dst) in enumerate(fixed):
+        copies.append(pltpu.make_async_copy(src, dst, fix_sems.at[i]))
+        copies[-1].start()
     load_corner.wait()
     for i in range(3):
         nodes[i : i + 1, : lay.depth] = corner[i, 0]
@@ -426,54 +418,42 @@
 
 def source_kernel(lay, *refs):
     extent, rows = lay.extent, lay.rows
-    own, upper, side, counts, plan, state, bulk, shear, radius, table, plane = refs[:11]
+    own, upper, side, counts_s, plan_s, state, plane, board = refs[:8]
     n = len(lay.near)
-    finished, first = refs[11:13]
-    others = refs[13 : 12 + n]
-    at = 12 + max(n, 1)
+    finished, first = refs[8:10]
+    others = refs[10 : 9 + n]
+    at = 9 + max(n, 1)
     boxes = refs[at : at + n]
-    counts_s, plan_s, small_sems, box_sems = refs[at + n : at + n + 4]
-    scratch = refs[at + n + 4 :]
-    small = [
-        pltpu.make_async_copy(counts, counts_s, small_sems.at[0]),
-        pltpu.make_async_copy(plan, plan_s, small_sems.at[1]),
-    ]
-    for copy in small:
-        copy.start()
+    box_sems = refs[at + n]
+    scratch = refs[at + n + 1 :]
     mask = lane_mask(rows)
     inside = jnp.where(lax.axis_index("rve") < lay.layers - 1, 1.0, 0.0)
     corners = [own[0:3], upper[0:3] * inside, side[0:3], side[8:11] * inside]
     strain = [to_column(v, mask) for v in strain_rows(corners)]
-    column = []
-
-    def late_counts():
-        for copy in small:
-            copy.wait()
-        values, top = counts_column(counts_s, rows)
-        column.append(values)
-        return values, top
-
-    sums = solve(
-        extent, rows, state, finished, strain, late_counts,
-        (bulk, shear, radius), (table, plane), scratch,
-    )
+    column, top = counts_column(counts_s, rows)
     away, order, target = lay.route(plan_s)
     stores = []
-    for i, offset in enumerate(lay.near):
-        for s in range(lay.late):
-            row, _ = lay.pick(away, order, offset, lay.early + s)
-            for tile in range(lay.wide // 128):
-                start = pl.multiple_of(row * lay.step, 8)
-                src = finished.at[tile, pl.ds(start, lay.step), :]
-                dst = boxes[i].at[s, :, pl.ds(tile * 128, 128)]
-                stores.append(pltpu.make_async_copy(src, dst, box_sems.at[i, s, tile]))
+
+    def ship(part):
+        span = pl.ds(part * (extent // 2), extent // 2)
+        for i, offset in enumerate(lay.near):
+            for s in range(lay.late):
+                row, _ = lay.pick(away, order, offset, lay.early + s)
+                src = finished.at[:, span, row, :]
+                dst = boxes[i].at[s, :, span, :]
+                stores.append(pltpu.make_async_copy(src, dst, box_sems.at[i, s, part]))
                 stores[-1].start()
+
+    sums = solve(
+        extent, rows, state, finished, strain, lambda: (column, top),
+        (board, plane), scratch, ship,
+    )
     lane = lax.broadcasted_iota(jnp.int32, (rows, 128), 1)
     sub = lax.broadcasted_iota(jnp.int32, (rows, 128), 0)
     card = jnp.zeros((rows, 128), jnp.float32)
     for c in range(6):
         card = jnp.where(lane == c, strain[c], card)
-    card = jnp.where(lane == 6, column[0], card)
+    card = jnp.where(lane == 6, column, card)
     for r in range(rows):
         label = (target[r] + 1).astype(jnp.float32)
         card = jnp.where(jnp.logical_and(lane == 7, sub == r), label, card)
@@ -503,18 +483,19 @@
 def target_kernel(lay, *refs):
     extent, rows, n = lay.extent, lay.rows, len(lay.near)
     notes, boxes = refs[:n], refs[n : 2 * n]
-    own, upper, bulk, shear, radius, table, plane = refs[2 * n : 2 * n + 7]
-    arrived, rare_out = refs[2 * n + 7 : 2 * n + 9]
-    rest = refs[2 * n + 9 :]
+    upper, plan_s, plane, board = refs[2 * n : 2 * n + 4]
+    arrived, rare_out, goals = refs[2 * n + 4 : 2 * n + 7]
+    rest = refs[2 * n + 7 :]
     marks, rest = rest[:n], rest[n:]
-    stage, result, load_sems, store_sems, mark_sems, cards = rest[:6]
-    scratch = rest[6:]
+    stage, result, load_sems, store_sems, mark_sems, cards, upper_s = rest[:7]
+    scratch = rest[7:]
     slots = [(i, s) for i in range(n) for s in range(lay.early)]
     reads = [pltpu.make_async_copy(notes[i], marks[i], mark_sems.at[i]) for i in range(n)]
+    reads.append(pltpu.make_async_copy(upper, upper_s, mark_sems.at[n]))
     loads = []
     for r, (i, s) in enumerate(slots):
-        for src, dst, sem in row_copies(boxes[i].at[s], stage, r, load_sems, extent):
-            loads.append(pltpu.make_async_copy(src, dst, sem))
+        dst = stage.at[:, :, r, :]
+        loads.append(pltpu.make_async_copy(boxes[i].at[s], dst, load_sems.at[r]))
     for copy in reads + loads:
         copy.start()
     cards[...] = jnp.zeros(cards.shape, jnp.float32)
@@ -529,18 +510,20 @@
         most = jnp.float32(0.0)
         for i, s in slots:
             most = jnp.maximum(most, marks[i][note_row(i, s), 6])
+        away, _, target = lay.route(plan_s)
+        for index, (i, s) in enumerate(lay.late_slots()):
+            goals[index] = marks[i][note_row(i, s), 7].astype(jnp.int32) - 1
+        for e in range(rows):
+            goals[n * lay.late + e] = jnp.where(away[e] == 0, target[e], -1)
+        rare = jnp.maximum(marks[0][note_row(0, 0), 8], marks[n - 1][note_row(n - 1, 0), 8])
+        rare_out[0] = jnp.where(jnp.maximum(rare, upper_s[3, 0]) > 0.0, 1, 0)
         return card[:, 6:7], most.astype(jnp.int32)
 
-    rare = jnp.maximum(own[3:4], upper[3:4])
-    for i in range(n):
-        flag = notes[i][note_row(i, 0) : note_row(i, 0) + 1]
-        rare = jnp.maximum(rare, jnp.broadcast_to(flag[:, 8:9], rare.shape))
-    rare_out[...] = jnp.broadcast_to(rare, rare_out.shape)
     for copy in loads:
         copy.wait()
     solve(
         extent, rows, stage, result, strain, late_counts,
-        (bulk, shear, radius), (table, plane), scratch,
+        (board, plane), scratch,
     )
     moves = []
     for r, (i, s) in enumerate(slots):
@@ -551,39 +534,24 @@
 
             @pl.when(valid)
             def _(r=r, where=where, phase=phase):
-                for dst, src, sem in row_copies(arrived.at[where], result, r, store_sems, extent):
-                    getattr(pltpu.make_async_copy(src, dst, sem), phase)()
+                src = result.at[:, :, r, :]
+                copy = pltpu.make_async_copy(src, arrived.at[where], store_sems.at[r])
+                getattr(copy, phase)()
 
 
 def place_kernel(lay, *refs):
     n = len(lay.near)
-    notes, boxes = refs[:n], refs[n : 2 * n]
-    plan, finished, _, out = refs[2 * n : 2 * n + 4]
-    marks, rest = refs[2 * n + 4 : 3 * n + 4], refs[3 * n + 4 :]
-    plan_s, mark_sems, box_sems, row_sems = rest
-    reads = [pltpu.make_async_copy(notes[i], marks[i], mark_sems.at[i]) for i in range(n)]
-    reads.append(pltpu.make_async_copy(plan, plan_s, mark_sems.at[n]))
-    for copy in reads:
-        copy.start()
-    for copy in reads:
-        copy.wait()
-    away, _, target = lay.route(plan_s)
-    moves = []
-    for i in range(n):
-        for s in range(lay.late):
-            label = marks[i][note_row(i, lay.early + s), 7].astype(jnp.int32)
-            where = jnp.maximum(label - 1, 0)
-            moves.append((label > 0, [(boxes[i].at[s], out.at[where], box_sems.at[i, s])]))
-    for e in range(lay.rows):
-        pieces = row_copies(out.at[target[e]], finished, e, row_sems, lay.extent)
-        moves.append((away[e] == 0, [(src, dst, sem) for dst, src, sem in pieces]))
+    goals, boxes = refs[0], refs[1 : n + 1]
+    finished, _, out, sems = refs[n + 1 :]
+    sources = [boxes[i].at[s - lay.early] for i, s in lay.late_slots()]
+    sources += [finished.at[:, :, e, :] for e in range(lay.rows)]
     for phase in ("start", "wait"):
-        for valid, pieces in moves:
-
-            @pl.when(valid)
-            def _(pieces=pieces, phase=phase):
-                for src, dst, sem in pieces:
-                    getattr(pltpu.make_async_copy(src, dst, sem), phase)()
+        for index, src in enumerate(sources):
+
+            @pl.when(goals[index] >= 0)
+            def _(index=index, src=src, phase=phase):
+                where = jnp.maximum(goals[index], 0)
+                getattr(pltpu.make_async_copy(src, out.at[where], sems.at[index]), phase)()
 
 
 def force_kernel(lay, own, below, side, out):
@@ -665,34 +633,36 @@
         lay.near = []
     rows, extent, wide, n = lay.rows, lay.extent, lay.wide, len(lay.near)
     f32 = jnp.float32
-    tiles = wide // 128
-    fixed = [bulk, shear, radius, jnp.asarray(symbol_table(extent)), jnp.asarray(plane_tables(extent))]
+    plane = jnp.asarray(plane_tables(extent))
+    fixed = [plane, jnp.asarray(symbol_table(extent)), bulk, shear, radius]
     vmem = pl.BlockSpec(memory_space=pltpu.VMEM)
     anywhere = pl.BlockSpec(memory_space=pl.ANY)
+    smem = pl.BlockSpec(memory_space=pltpu.SMEM)
     sem = pltpu.SemaphoreType.DMA
     params = pltpu.CompilerParams(vmem_limit_bytes=VMEM_BYTES)
-    staging = pltpu.VMEM((tiles, rows * lay.step, 128), f32)
+    staging = pltpu.VMEM(lay.field, f32)
     small = pltpu.SMEM((rows,), jnp.int32)
     plan = in_hbm(migration_plan)
     nodes, state, *rest = pl.pallas_call(
         lambda *refs: pack_kernel(lay, *refs),
         out_shape=[pltpu.VMEM((8, 128), f32), staging]
-        + [pltpu.VMEM(v.shape, v.dtype) for v in fixed]
-        + [pltpu.VMEM((lay.early, lay.step, wide), f32)] * n,
-        in_specs=[anywhere] * 8,
-        out_specs=[vmem] * (7 + n),
+        + [pltpu.VMEM(plane.shape, plane.dtype), pltpu.VMEM((len(SYM) + 3, extent, wide), f32)]
+        + [small, small]
+        + [pltpu.VMEM((lay.early,) + lay.row, f32)] * n,
+        in_specs=[anywhere] * 9,
+        out_specs=[vmem] * 4 + [smem] * 2 + [vmem] * n,
         scratch_shapes=[
-            small,
             pltpu.VMEM(displacement.shape, f32),
-            sem((2,)),
+            sem((3,)),
             sem((max(n, 1), max(lay.early, 1))),
             sem((5,)),
-            sem((rows, tiles)),
+            sem((rows,)),
         ],
         name="pack",
-    )(in_hbm(displacement), plan, in_hbm(plastic.reshape(rows, lay.step, wide)), *[in_hbm(v) for v in fixed])
-    fixed = [in_vmem(v) for v in rest[:5]]
-    raw = rest[5:]
+    )(in_hbm(displacement), plan, in_hbm(counts), in_hbm(plastic), *[in_hbm(v) for v in fixed])
+    fixed = [in_vmem(v) for v in rest[:2]]
+    plan, counts = [pltpu.with_memory_space_constraint(v, pltpu.SMEM) for v in rest[2:4]]
+    raw = rest[4:]
     upper = ring(nodes, -1)
     for i, offset in enumerate(lay.near):
         raw[i] = ring(raw[i], offset)
@@ -701,17 +671,17 @@
     nodes, upper = in_vmem(nodes), in_vmem(upper)
     outs = [staging, pltpu.VMEM((8 + lay.meta, 128), f32)]
     outs += [pltpu.VMEM((lay.meta, 128), f32)] * (n - 1)
-    outs += [pltpu.VMEM((lay.late, lay.step, wide), f32)] * n
+    outs += [pltpu.HBM((lay.late,) + lay.row, f32)] * n
     finished, *rest = pl.pallas_call(
         lambda *refs: source_kernel(lay, *refs),
         out_shape=outs,
-        in_specs=[vmem] * 3 + [anywhere] * 2 + [vmem] * 6,
-        out_specs=[vmem] * len(outs),
-        scratch_shapes=[small, small, sem((2,)), sem((max(n, 1), max(lay.late, 1), tiles))]
+        in_specs=[vmem] * 3 + [smem] * 2 + [vmem] * 3,
+        out_specs=[vmem] * (1 + max(n, 1)) + [anywhere] * n,
+        scratch_shapes=[sem((max(n, 1), max(lay.late, 1), 2))]
         + solve_scratch(extent, rows),
         compiler_params=params,
         name="solve_source",
-    )(nodes, upper, in_vmem(side), in_hbm(counts), plan, in_vmem(state), *fixed)
+    )(nodes, upper, in_vmem(side), counts, plan, in_vmem(state), *fixed)
     first, others, done = rest[0], rest[1:n], rest[max(n, 1) :]
     below = ring(first, 1)
     notes = [below]
@@ -730,38 +700,41 @@
     )(in_vmem(first), in_vmem(below), in_vmem(beside))
 
     def unusual(_):
-        rows_first = finished.reshape(tiles, rows, lay.step, 128).transpose(1, 2, 0, 3)
-        return move_any(rows_first.reshape(rows, lay.step, wide), migration_plan)
+        return move_any(finished.transpose(2, 0, 1, 3), migration_plan)
 
     if not fast:
-        return force, unusual(None).reshape(plastic.shape)
+        return force, unusual(None)
     notes = [in_vmem(v) for v in notes]
-    marks = [pltpu.SMEM(v.shape, f32) for v in notes]
-    arrived, rare = pl.pallas_call(
+    total = n * lay.late + rows
+    arrived, rare, goals = pl.pallas_call(
         lambda *refs: target_kernel(lay, *refs),
-        out_shape=[pltpu.HBM((rows, lay.step, wide), f32), jax.ShapeDtypeStruct((8, 128), f32)],
-        in_specs=[vmem] * n + [vmem] * n + [vmem] * 7,
-        out_specs=[anywhere, vmem],
-        scratch_shapes=marks
-        + [staging, staging, sem((rows, tiles)), sem((rows, tiles)), sem((n,))]
-        + [pltpu.VMEM((rows, 128), f32)]
+        out_shape=[
+            pltpu.HBM(plastic.shape, f32),
+            pltpu.SMEM((1,), jnp.int32),
+            pltpu.SMEM((total,), jnp.int32),
+        ],
+        in_specs=[vmem] * (2 * n + 1) + [smem] + [vmem] * 2,
+        out_specs=[anywhere, smem, smem],
+        scratch_shapes=[pltpu.SMEM(v.shape, f32) for v in notes]
+        + [staging, staging, sem((rows,)), sem((rows,)), sem((n + 1,))]
+        + [pltpu.VMEM((rows, 128), f32), pltpu.SMEM((8, 128), f32)]
         + solve_scratch(extent, rows),
         compiler_params=params,
         name="solve_target",
-    )(*notes, *[in_vmem(v) for v in raw], nodes, upper, *fixed)
+    )(*notes, *[in_vmem(v) for v in raw], upper, plan, *fixed)
+    goals = pltpu.with_memory_space_constraint(goals, pltpu.SMEM)
     moved = pl.pallas_call(
         lambda *refs: place_kernel(lay, *refs),
-        out_shape=pltpu.HBM((rows, lay.step, wide), f32),
-        in_specs=[vmem] * (2 * n) + [anywhere, vmem, anywhere],
+        out_shape=pltpu.HBM(plastic.shape, f32),
+        in_specs=[smem] + [vmem] * (n + 1) + [anywhere],
         out_specs=anywhere,
-        scratch_shapes=marks
-        + [small, sem((n + 1,)), sem((n, lay.late)), sem((rows, tiles))],
-        input_output_aliases={2 * n + 2: 0},
+        scratch_shapes=[sem((total,))],
+        input_output_aliases={n + 2: 0},
         compiler_params=params,
         name="place",
-    )(*notes, *[in_vmem(v) for v in done], plan, in_vmem(finished), in_hbm(arrived))
-    moved = lax.cond(rare[0, 0] > 0.0, unusual, lambda v: v, moved)
-    return force, moved.reshape(plastic.shape)
+    )(goals, *[in_vmem(v) for v in done], in_vmem(finished), in_hbm(arrived))
+    moved = lax.cond(rare[0] > 0, unusual, lambda v: v, moved)
+    return force, moved
 
 
 def solution(mesh):

time: 60.3 us -> 57.1 us (0.947)
  Pallas kernels: 18.6 us -> 15.9 us
  between operations: 1.34 us -> 0.73 us
    pallas_call x1, Pallas kernels: 1.82 us -> 0.86 us  [on_device(): pl.pallas_call(lambda *refs: place_kernel(lay, *refs), out_shape=pltpu.HB...]
    pallas_call x1, Pallas kernels: 2.99 us -> 2.28 us  [on_device(): pl.pallas_call(lambda *refs: pack_kernel(lay, *refs), out_shape=[pltpu.VM...]
  transfers between devices with their start and end apart: 9 -> 9, of which waited for: 4 -> 4; matrix products, arithmetic and copies ran while one was open for 1% -> 0% of each run, Pallas kernels for 23% -> 23%
where the time goes in v1:
time: 57.1 us; the launch traced here: 56.8 us
  waiting for transfers between devices  24.1 us (42%)
  starting transfers between devices  16 us (28%)
  Pallas kernels  15.9 us (28%)
  between operations  0.73 us (1%)
    ppermute x7, waiting for transfers between devices, ring(): lax.ppermute(value, 'rve', [(i, (i + step) % layers) for i in range(layer...  20.1 us
    ppermute x7, starting transfers between devices, ring(): lax.ppermute(value, 'rve', [(i, (i + step) % layers) for i in range(layer...  12.2 us
    pallas_call x1, Pallas kernels, on_device(): pl.pallas_call(lambda *refs: target_kernel(lay, *refs), out_shape=[pltpu....  8.13 us
    pallas_call x1, Pallas kernels, on_device(): pl.pallas_call(lambda *refs: source_kernel(lay, *refs), out_shape=outs, i...  4.03 us
    ppermute x2, waiting for transfers between devices, sideways(): return lax.ppermute(value, ('mic', 'mac'), shift_pairs([columns], [step]))  3.94 us
    ppermute x2, starting transfers between devices, sideways(): return lax.ppermute(value, ('mic', 'mac'), shift_pairs([columns], [step]))  3.82 us
    pallas_call x1, Pallas kernels, on_device(): pl.pallas_call(lambda *refs: pack_kernel(lay, *refs), out_shape=[pltpu.VM...  2.28 us
  transfers between devices with their start and end apart: 9, of which 4 were waited for; matrix products, arithmetic and copies ran while one was open for 0% of the time, Pallas kernels for 23%

profile of v1, /device:TPU:20, one launch (start us, length us, event | category | flops | bytes accessed | tf_op | source)
XLA Modules:
  0.0 56.8 jit_solution(8963252644723816547)
XLA Ops:
  0.6 2.3 %pack.1 = (f32[8,128]{1,0:T(8,128)S(1)}, f32[6,16,8,256]{3,2,1,0:T(8,128)S(1)}, bf16[2,768,256]{2,1,0:T(8,128)(2,1)S(1)}, f32[24,16,256]{2,1,0:T(8,128)S(1)}, s3...) custom-call(f32[3,1,1,8]{3,2,1,0:T(1,128)} %refs_0_.1, s32[8]{0:T(128)} %refs_1_.1, ...), custom_call_target="tpu_custom_call" | custom-call | tf_op jit(solution)/shard_map/pack/pallas_call | solution.py:646
  2.9 0.5 collective-permute-start
  3.4 3.2 %collective-permute-done.refs_1_.refs_4_ = f32[8,128]{1,0:T(8,128)S(1)} collective-permute-done((f32[8,128]{1,0:T(8,128)S(1)}, f32[8,128]{1,0:T(8,128)S(1)}, u32[]{:S(2)}, u32[]{:S(2)}) %collective-permute-start) | collective-permute-done | bytes 4128 | tf_op jit(solution)/shard_map/ppermute | solution.py:582
  6.6 1.9 %collective-permute-start.1 = (f32[16,128]{1,0:T(8,128)S(1)}, f32[16,128]{1,0:T(8,128)S(1)}, u32[]{:S(2)}, u32[]{:S(2)}) collective-permute-start(f32[16,128]{1,0:T(8,128)S(1)} %pad_maximum_fusion), channel_id=1, source_target_pairs={{1,0},{2,1},{3,2},{4,3},{5,4},{6,5},{7,6},{9,8},{10,9},{11,10},{12... | collective-permute-start | bytes 24584 | tf_op jit(solution)/shard_map/ppermute | solution.py:587
  8.5 3.4 %collective-permute-start.5 = (f32[2,6,16,256]{3,2,1,0:T(8,128)S(1)}, f32[2,6,16,256]{3,2,1,0:T(8,128)S(1)}, u32[]{:S(2)}, u32[]{:S(2)}) collective-permute-start(f32[2,6,16,256]{3,2,1,0:T(8,128)S(1)} %get-tuple-element.36), channel_id=1, source_target_pairs={{0,8},{8,16},{16,24},{24,0},{1,9},{9,17},{17,25},{25,1},{2,10},{10... | collective-permute-start | bytes 589832 | tf_op jit(solution)/shard_map/ppermute | solution.py:582
  11.9 0.0 collective-permute-start.6
  11.9 0.0 collective-permute-done.1.refs_2_
  11.9 4.0 %solve_source.1 = (f32[6,16,8,256]{3,2,1,0:T(8,128)S(1)}, f32[16,128]{1,0:T(8,128)S(1)}, f32[8,128]{1,0:T(8,128)}, f32[2,6,16,256]{3,2,1,0:T(8,128)}, f32[2,6,16,256]{3,2,1,0:T(8,128)}) custom-call(f32[8,128]{1,0:T(8,128)S(1)} %get-tuple-element.28.refs_0_, f32[8,128]{1,0:T(8,128)S(1)} %collective-permute-done.refs_1_.refs_4_, ...), custom_call_target="tpu_custom_call" | custom-call | tf_op jit(solution)/shard_map/solve_source/pallas_call | solution.py:675
  16.0 1.3 %collective-permute-start.7 = (f32[2,6,16,256]{3,2,1,0:T(8,128)}, f32[2,6,16,256]{3,2,1,0:T(8,128)S(1)}, u32[]{:S(2)}, u32[]{:S(2)}) collective-permute-start(f32[2,6,16,256]{3,2,1,0:T(8,128)} %get-tuple-element.40), channel_id=1, source_target_pairs={{0,8},{8,16},{16,24},{24,0},{1,9},{9,17},{17,25},{25,1},{2,10},{10... | collective-permute-start | bytes 589832 | tf_op jit(solution)/shard_map/ppermute | solution.py:582
  17.3 5.6 %collective-permute-start.8 = (f32[2,6,16,256]{3,2,1,0:T(8,128)}, f32[2,6,16,256]{3,2,1,0:T(8,128)S(1)}, u32[]{:S(2)}, u32[]{:S(2)}) collective-permute-start(f32[2,6,16,256]{3,2,1,0:T(8,128)} %get-tuple-element.41), channel_id=1, source_target_pairs={{0,16},{8,24},{16,0},{24,8},{1,17},{9,25},{17,1},{25,9},{2,18},{10... | collective-permute-start | bytes 589832 | tf_op jit(solution)/shard_map/ppermute | solution.py:582
  22.9 1.4 %collective-permute-start.2 = (f32[16,128]{1,0:T(8,128)S(1)}, f32[16,128]{1,0:T(8,128)S(1)}, u32[]{:S(2)}, u32[]{:S(2)}) collective-permute-start(f32[16,128]{1,0:T(8,128)S(1)} %get-tuple-element.34.refs_0_), channel_id=1, source_target_pairs={{0,8},{8,16},{16,24},{24,0},{1,9},{9,17},{17,25},{25,1},{2,10},{10... | collective-permute-start | bytes 24584 | tf_op jit(solution)/shard_map/ppermute | solution.py:582
  24.3 12.9 %collective-permute-done.2.refs_1_.refs_0_ = f32[16,128]{1,0:T(8,128)S(1)} collective-permute-done((f32[16,128]{1,0:T(8,128)S(1)}, f32[16,128]{1,0:T(8,128)S(1)}, u32[]{:S(2)}, u32[]{:S(2)}) %collective-permute-start.2) | collective-permute-done | bytes 8224 | tf_op jit(solution)/shard_map/ppermute | solution.py:582
  37.2 1.9 %collective-permute-start.3 = (f32[16,128]{1,0:T(8,128)S(1)}, f32[16,128]{1,0:T(8,128)S(1)}, u32[]{:S(2)}, u32[]{:S(2)}) collective-permute-start(f32[16,128]{1,0:T(8,128)S(1)} %pad_maximum_fusion.1), channel_id=1, source_target_pairs={{0,1},{1,2},{2,3},{3,4},{4,5},{5,6},{6,7},{8,9},{9,10},{10,11},{11... | collective-permute-start | bytes 24584 | tf_op jit(solution)/shard_map/ppermute | solution.py:587
  39.1 3.9 %collective-permute-done.3.refs_2_ = f32[16,128]{1,0:T(8,128)S(1)} collective-permute-done((f32[16,128]{1,0:T(8,128)S(1)}, f32[16,128]{1,0:T(8,128)S(1)}, u32[]{:S(2)}, u32[]{:S(2)}) %collective-permute-start.3) | collective-permute-done | bytes 8224 | tf_op jit(solution)/shard_map/ppermute | solution.py:587
  43.1 0.0 collective-permute-start.4
  43.1 0.6 %force.1 = f32[3,1,1,8]{3,2,1,0:T(1,128)} custom-call(f32[16,128]{1,0:T(8,128)S(1)} %get-tuple-element.34.refs_0_, f32[16,128]{1,0:T(8,128)S(1)} %collective-permute-done.2.refs_1_.refs_0_, f32[16,128]{1,0:T(8,128)S(1)} %collective-permute-done.3.refs_2_), custom_call_target="tpu_custom_call" | custom-call | tf_op jit(solution)/shard_map/force/pallas_call | solution.py:694
  43.7 4.1 %collective-permute-done.4.refs_1_ = f32[8,128]{1,0:T(8,128)S(1)} collective-permute-done((f32[8,128]{1,0:T(8,128)}, f32[8,128]{1,0:T(8,128)S(1)}, u32[]{:S(2)}, u32[]{:S(2)}) %collective-permute-start.4) | collective-permute-done | bytes 4128 | tf_op jit(solution)/shard_map/ppermute | solution.py:582
  47.8 0.0 collective-permute-done.5.refs_2_
  47.8 0.0 collective-permute-done.6.refs_3_
  47.8 8.1 %solve_target.1 = (f32[8,6,16,256]{3,2,1,0:T(8,128)}, s32[1]{0:T(128)S(4)}, s32[12]{0:T(128)S(4)}) custom-call(f32[16,128]{1,0:T(8,128)S(1)} %collective-permute-done.2.refs_1_.refs_0_, f32[8,128]{1,0:T(8,128)S(1)} %collective-permute-done.4.refs_1_, f32[2,6,16,256]{3,2,1,0:T(8,128)S(1)} %collective-permute-done.5.refs_2_, ...), custom_call_target="tpu_custom_call" | custom-call | tf_op jit(solution)/shard_map/solve_target/pallas_call | solution.py:709
  55.9 0.0 copy-start
  55.9 0.0 collective-permute-done.7.refs_1_
  55.9 0.0 collective-permute-done.8.refs_2_
  56.0 0.9 %place.1 = f32[8,6,16,256]{3,2,1,0:T(8,128)} custom-call(s32[12]{0:T(128)S(4)} %get-tuple-element.39.refs_0_, f32[2,6,16,256]{3,2,1,0:T(8,128)S(1)} %collective-permute-done.7.refs_1_, f32[2,6,16,256]{3,2,1,0:T(8,128)S(1)} %collective-permute-done.8.refs_2_, f32[6,16,8,256]{3,2,1,0:T(8,128)S(1)} %get-tuple-element.42.refs_3_, ...), custom_call_target="tpu_custom_call", output_to_operand_aliasing={{}: (4, {})} | custom-call | tf_op jit(solution)/shard_map/place/pallas_call | solution.py:726
  56.8 0.0 copy-done
  (5 shorter events, 0.0 us)
Async XLA Ops:
  2.9 3.7 %collective-permute-start = (f32[8,128]{1,0:T(8,128)S(1)}, f32[8,128]{1,0:T(8,128)S(1)}, u32[]{:S(2)}, u32[]{:S(2)}) collective-permute-start(f32[8,128]{1,0:T(8,128)S(1)} %get-tuple-element.28.refs_0_), channel_id=1, source_target_pairs={{0,24},{8,0},{16,8},{24,16},{1,25},{9,1},{17,9},{25,17},{2,26},{10... | collective-permute-start | bytes 12296 | tf_op jit(solution)/shard_map/ppermute | solution.py:582
  6.6 5.3 %collective-permute-start.1 = (f32[16,128]{1,0:T(8,128)S(1)}, f32[16,128]{1,0:T(8,128)S(1)}, u32[]{:S(2)}, u32[]{:S(2)}) collective-permute-start(f32[16,128]{1,0:T(8,128)S(1)} %pad_maximum_fusion), channel_id=1, source_target_pairs={{1,0},{2,1},{3,2},{4,3},{5,4},{6,5},{7,6},{9,8},{10,9},{11,10},{12... | collective-permute-start | bytes 24584 | tf_op jit(solution)/shard_map/ppermute | solution.py:587
  8.5 39.3 %collective-permute-start.5 = (f32[2,6,16,256]{3,2,1,0:T(8,128)S(1)}, f32[2,6,16,256]{3,2,1,0:T(8,128)S(1)}, u32[]{:S(2)}, u32[]{:S(2)}) collective-permute-start(f32[2,6,16,256]{3,2,1,0:T(8,128)S(1)} %get-tuple-element.36), channel_id=1, source_target_pairs={{0,8},{8,16},{16,24},{24,0},{1,9},{9,17},{17,25},{25,1},{2,10},{10... | collective-permute-start | bytes 589832 | tf_op jit(solution)/shard_map/ppermute | solution.py:582
  11.9 35.8 %collective-permute-start.6 = (f32[2,6,16,256]{3,2,1,0:T(8,128)S(1)}, f32[2,6,16,256]{3,2,1,0:T(8,128)S(1)}, u32[]{:S(2)}, u32[]{:S(2)}) collective-permute-start(f32[2,6,16,256]{3,2,1,0:T(8,128)S(1)} %get-tuple-element.37), channel_id=1, source_target_pairs={{0,16},{8,24},{16,0},{24,8},{1,17},{9,25},{17,1},{25,9},{2,18},{10... | collective-permute-start | bytes 589832 | tf_op jit(solution)/shard_map/ppermute | solution.py:582
  16.0 40.0 %collective-permute-start.7 = (f32[2,6,16,256]{3,2,1,0:T(8,128)}, f32[2,6,16,256]{3,2,1,0:T(8,128)S(1)}, u32[]{:S(2)}, u32[]{:S(2)}) collective-permute-start(f32[2,6,16,256]{3,2,1,0:T(8,128)} %get-tuple-element.40), channel_id=1, source_target_pairs={{0,8},{8,16},{16,24},{24,0},{1,9},{9,17},{17,25},{25,1},{2,10},{10... | collective-permute-start | bytes 589832 | tf_op jit(solution)/shard_map/ppermute | solution.py:582
  17.3 38.6 %collective-permute-start.8 = (f32[2,6,16,256]{3,2,1,0:T(8,128)}, f32[2,6,16,256]{3,2,1,0:T(8,128)S(1)}, u32[]{:S(2)}, u32[]{:S(2)}) collective-permute-start(f32[2,6,16,256]{3,2,1,0:T(8,128)} %get-tuple-element.41), channel_id=1, source_target_pairs={{0,16},{8,24},{16,0},{24,8},{1,17},{9,25},{17,1},{25,9},{2,18},{10... | collective-permute-start | bytes 589832 | tf_op jit(solution)/shard_map/ppermute | solution.py:582
  22.9 14.3 %collective-permute-start.2 = (f32[16,128]{1,0:T(8,128)S(1)}, f32[16,128]{1,0:T(8,128)S(1)}, u32[]{:S(2)}, u32[]{:S(2)}) collective-permute-start(f32[16,128]{1,0:T(8,128)S(1)} %get-tuple-element.34.refs_0_), channel_id=1, source_target_pairs={{0,8},{8,16},{16,24},{24,0},{1,9},{9,17},{17,25},{25,1},{2,10},{10... | collective-permute-start | bytes 24584 | tf_op jit(solution)/shard_map/ppermute | solution.py:582
  37.2 5.9 %collective-permute-start.3 = (f32[16,128]{1,0:T(8,128)S(1)}, f32[16,128]{1,0:T(8,128)S(1)}, u32[]{:S(2)}, u32[]{:S(2)}) collective-permute-start(f32[16,128]{1,0:T(8,128)S(1)} %pad_maximum_fusion.1), channel_id=1, source_target_pairs={{0,1},{1,2},{2,3},{3,4},{4,5},{5,6},{6,7},{8,9},{9,10},{10,11},{11... | collective-permute-start | bytes 24584 | tf_op jit(solution)/shard_map/ppermute | solution.py:587
  43.1 4.7 %collective-permute-start.4 = (f32[8,128]{1,0:T(8,128)}, f32[8,128]{1,0:T(8,128)S(1)}, u32[]{:S(2)}, u32[]{:S(2)}) collective-permute-start(f32[8,128]{1,0:T(8,128)} %get-tuple-element.35), channel_id=1, source_target_pairs={{0,16},{8,24},{16,0},{24,8},{1,17},{9,25},{17,1},{25,9},{2,18},{10... | collective-permute-start | bytes 12296 | tf_op jit(solution)/shard_map/ppermute | solution.py:582
  55.9 0.9 %copy-start = (s32[8]{0:T(128)S(1)}, s32[8]{0:T(128)}, u32[]{:S(2)}) copy-start(s32[8]{0:T(128)} %refs_1_.1) | copy-start | bytes 100

commit v2 on v1

--- a/solution.py
+++ b/solution.py
@@ -12,6 +12,7 @@
 COUPLING = 0.7
 EARLY = 2
 VMEM_BYTES = 20 * 2**20
+SMALL_BYTES = 8 * 2**20
 PAIRS = [(0, 0), (1, 1), (2, 2), (1, 2), (0, 2), (0, 1)]
 SYM = [(m, n) for m in range(6) for n in range(m, 6)]
 
@@ -375,19 +376,15 @@
 
 def pack_kernel(lay, *refs):
     displacement, plan, counts, plastic = refs[:4]
-    plane, table, *fields = refs[4:9]
-    nodes, state, plane_copy, board, plan_s, counts_s = refs[9:15]
-    boxes = refs[15 : 15 + len(lay.near)]
-    corner, small_sems, box_sems, fix_sems, row_sems = refs[15 + len(lay.near) :]
+    nodes, plan_s, counts_s = refs[4:7]
+    boxes = refs[7 : 7 + len(lay.near)]
+    corner, small_sems, box_sems = refs[7 + len(lay.near) :]
     load_plan = pltpu.make_async_copy(plan, plan_s, small_sems.at[0])
     load_plan.start()
     load_corner = pltpu.make_async_copy(displacement, corner, small_sems.at[1])
     load_corner.start()
-    copies = [pltpu.make_async_copy(counts, counts_s, small_sems.at[2])]
-    copies[0].start()
-    for r in range(lay.rows):
-        copies.append(pltpu.make_async_copy(plastic.at[r], state.at[:, :, r, :], row_sems.at[r]))
-        copies[-1].start()
+    load_counts = pltpu.make_async_copy(counts, counts_s, small_sems.at[2])
+    load_counts.start()
     nodes[...] = jnp.zeros(nodes.shape, jnp.float32)
     load_plan.wait()
     away, order, _ = lay.route(plan_s)
@@ -397,11 +394,6 @@
             row, _ = lay.pick(away, order, offset, s)
             packed.append(pltpu.make_async_copy(plastic.at[row], boxes[i].at[s], box_sems.at[i, s]))
             packed[-1].start()
-    fixed = [(plane, plane_copy), (table, board.at[pl.ds(0, len(SYM))])]
-    fixed += [(field, board.at[len(SYM) + i]) for i, field in enumerate(fields)]
-    for i, (src, dst) in enumerate(fixed):
-        copies.append(pltpu.make_async_copy(src, dst, fix_sems.at[i]))
-        copies[-1].start()
     load_corner.wait()
     for i in range(3):
         nodes[i : i + 1, : lay.depth] = corner[i, 0]
@@ -412,7 +404,25 @@
             usual = jnp.logical_or(usual, away[e] == offset)
         rare = jnp.where(usual, rare, 1)
     nodes[3:4] = jnp.full((1, 128), rare.astype(jnp.float32))
-    for copy in copies + packed:
+    load_counts.wait()
+    for copy in packed:
+        copy.wait()
+
+
+def load_kernel(lay, *refs):
+    plastic, plane, table, *fields = refs[:6]
+    state, plane_copy, board = refs[6:9]
+    fix_sems, row_sems = refs[9:]
+    copies = []
+    for r in range(lay.rows):
+        copies.append(pltpu.make_async_copy(plastic.at[r], state.at[:, :, r, :], row_sems.at[r]))
+    fixed = [(plane, plane_copy), (table, board.at[pl.ds(0, len(SYM))])]
+    fixed += [(field, board.at[len(SYM) + i]) for i, field in enumerate(fields)]
+    for i, (src, dst) in enumerate(fixed):
+        copies.append(pltpu.make_async_copy(src, dst, fix_sems.at[i]))
+    for copy in copies:
+        copy.start()
+    for copy in copies:
         copy.wait()
 
 
@@ -542,16 +552,22 @@
 def place_kernel(lay, *refs):
     n = len(lay.near)
     goals, boxes = refs[0], refs[1 : n + 1]
-    finished, _, out, sems = refs[n + 1 :]
+    own, below, beside, finished, _, out, force, line, sems, line_sem = refs[n + 1 :]
     sources = [boxes[i].at[s - lay.early] for i, s in lay.late_slots()]
     sources += [finished.at[:, :, e, :] for e in range(lay.rows)]
     for phase in ("start", "wait"):
+        if phase == "wait":
+            force_kernel(lay, own, below, beside, line)
+            send = pltpu.make_async_copy(line, force, line_sem)
+            send.start()
         for index, src in enumerate(sources):
 
             @pl.when(goals[index] >= 0)
             def _(index=index, src=src, phase=phase):
                 where = jnp.maximum(goals[index], 0)
                 getattr(pltpu.make_async_copy(src, out.at[where], sems.at[index]), phase)()
+
+    send.wait()
 
 
 def force_kernel(lay, own, below, side, out):
@@ -643,26 +659,35 @@
     staging = pltpu.VMEM(lay.field, f32)
     small = pltpu.SMEM((rows,), jnp.int32)
     plan = in_hbm(migration_plan)
-    nodes, state, *rest = pl.pallas_call(
+    nodes, plan, counts, *raw = pl.pallas_call(
         lambda *refs: pack_kernel(lay, *refs),
-        out_shape=[pltpu.VMEM((8, 128), f32), staging]
-        + [pltpu.VMEM(plane.shape, plane.dtype), pltpu.VMEM((len(SYM) + 3, extent, wide), f32)]
-        + [small, small]
+        out_shape=[pltpu.VMEM((8, 128), f32), small, small]
         + [pltpu.VMEM((lay.early,) + lay.row, f32)] * n,
-        in_specs=[anywhere] * 9,
-        out_specs=[vmem] * 4 + [smem] * 2 + [vmem] * n,
+        in_specs=[anywhere] * 4,
+        out_specs=[vmem] + [smem] * 2 + [vmem] * n,
         scratch_shapes=[
             pltpu.VMEM(displacement.shape, f32),
             sem((3,)),
             sem((max(n, 1), max(lay.early, 1))),
-            sem((5,)),
-            sem((rows,)),
         ],
+        compiler_params=pltpu.CompilerParams(vmem_limit_bytes=SMALL_BYTES),
         name="pack",
-    )(in_hbm(displacement), plan, in_hbm(counts), in_hbm(plastic), *[in_hbm(v) for v in fixed])
-    fixed = [in_vmem(v) for v in rest[:2]]
-    plan, counts = [pltpu.with_memory_space_constraint(v, pltpu.SMEM) for v in rest[2:4]]
-    raw = rest[4:]
+    )(in_hbm(displacement), plan, in_hbm(counts), in_hbm(plastic))
+    plan, counts = [pltpu.with_memory_space_constraint(v, pltpu.SMEM) for v in (plan, counts)]
+    state, *fixed = pl.pallas_call(
+        lambda *refs: load_kernel(lay, *refs),
+        out_shape=[
+            staging,
+            pltpu.VMEM(plane.shape, plane.dtype),
+            pltpu.VMEM((len(SYM) + 3, extent, wide), f32),
+        ],
+        in_specs=[anywhere] * 6,
+        out_specs=[vmem] * 3,
+        scratch_shapes=[sem((5,)), sem((rows,))],
+        compiler_params=pltpu.CompilerParams(vmem_limit_bytes=SMALL_BYTES),
+        name="load",
+    )(in_hbm(plastic), *[in_hbm(v) for v in fixed])
+    fixed = [in_vmem(v) for v in fixed]
     upper = ring(nodes, -1)
     for i, offset in enumerate(lay.near):
         raw[i] = ring(raw[i], offset)
@@ -691,18 +716,20 @@
         done[i] = ring(done[i], offset)
     pair = jnp.concatenate([first[:8], below[:8]], axis=0)
     beside = sideways(pair, 1)
-    force = pl.pallas_call(
-        lambda *refs: force_kernel(lay, *refs),
-        out_shape=jax.ShapeDtypeStruct(displacement.shape, f32),
-        in_specs=[vmem] * 3,
-        out_specs=vmem,
-        name="force",
-    )(in_vmem(first), in_vmem(below), in_vmem(beside))
 
     def unusual(_):
         return move_any(finished.transpose(2, 0, 1, 3), migration_plan)
 
+    sides = [in_vmem(v) for v in (first, below, beside)]
     if not fast:
+        force = pl.pallas_call(
+            lambda *refs: force_kernel(lay, *refs),
+            out_shape=jax.ShapeDtypeStruct(displacement.shape, f32),
+            in_specs=[vmem] * 3,
+            out_specs=vmem,
+            compiler_params=pltpu.CompilerParams(vmem_limit_bytes=SMALL_BYTES),
+            name="force",
+        )(*sides)
         return force, unusual(None)
     notes = [in_vmem(v) for v in notes]
     total = n * lay.late + rows
@@ -723,16 +750,16 @@
         name="solve_target",
     )(*notes, *[in_vmem(v) for v in raw], upper, plan, *fixed)
     goals = pltpu.with_memory_space_constraint(goals, pltpu.SMEM)
-    moved = pl.pallas_call(
+    moved, force = pl.pallas_call(
         lambda *refs: place_kernel(lay, *refs),
-        out_shape=pltpu.HBM(plastic.shape, f32),
-        in_specs=[smem] + [vmem] * (n + 1) + [anywhere],
-        out_specs=anywhere,
-        scratch_shapes=[sem((total,))],
-        input_output_aliases={n + 2: 0},
+        out_shape=[pltpu.HBM(plastic.shape, f32), pltpu.HBM(displacement.shape, f32)],
+        in_specs=[smem] + [vmem] * (n + 4) + [anywhere],
+        out_specs=[anywhere] * 2,
+        scratch_shapes=[pltpu.VMEM(displacement.shape, f32), sem((total,)), sem(())],
+        input_output_aliases={n + 5: 0},
         compiler_params=params,
         name="place",
-    )(goals, *[in_vmem(v) for v in done], in_vmem(finished), in_hbm(arrived))
+    )(goals, *[in_vmem(v) for v in done], *sides, in_vmem(finished), in_hbm(arrived))
     moved = lax.cond(rare[0] > 0, unusual, lambda v: v, moved)
     return force, moved
 

time: 57.1 us -> 54.1 us (0.947)
  the two profiles are of different devices: /device:TPU:20 before, /device:TPU:17 now
where the time goes in v2:
time: 54.1 us; the launch traced here: 53.8 us
  waiting for transfers between devices  19 us (35%)
  starting transfers between devices  18.3 us (34%)
  Pallas kernels  15.8 us (29%)
  between operations  0.76 us (1%)
    ppermute x7, waiting for transfers between devices, ring(): lax.ppermute(value, 'rve', [(i, (i + step) % layers) for i in range(layer...  19 us
    ppermute x7, starting transfers between devices, ring(): lax.ppermute(value, 'rve', [(i, (i + step) % layers) for i in range(layer...  9.77 us
    ppermute x2, starting transfers between devices, sideways(): return lax.ppermute(value, ('mic', 'mac'), shift_pairs([columns], [step]))  8.51 us
    pallas_call x1, Pallas kernels, on_device(): pl.pallas_call(lambda *refs: target_kernel(lay, *refs), out_shape=[pltpu....  7.96 us
    pallas_call x1, Pallas kernels, on_device(): pl.pallas_call(lambda *refs: source_kernel(lay, *refs), out_shape=outs, i...  3.41 us
    pallas_call x1, Pallas kernels, on_device(): pl.pallas_call(lambda *refs: pack_kernel(lay, *refs), out_shape=[pltpu.VM...  1.83 us
    pallas_call x1, Pallas kernels, on_device(): pl.pallas_call(lambda *refs: load_kernel(lay, *refs), out_shape=[staging,...  1.68 us
  transfers between devices with their start and end apart: 9, of which 3 were waited for; matrix products, arithmetic and copies ran while one was open for 0% of the time, Pallas kernels for 24%

profile of v2, /device:TPU:17, one launch (start us, length us, event | category | flops | bytes accessed | tf_op | source)
XLA Modules:
  0.0 53.8 jit_solution(11072652937681866586)
XLA Ops:
  0.6 1.8 %pack.1 = (f32[8,128]{1,0:T(8,128)S(1)}, s32[8]{0:T(128)S(4)}, s32[8]{0:T(128)S(4)}, f32[2,6,16,256]{3,2,1,0:T(8,128)S(1)}, f32[2,6,16,256]{3,2,1,0:T(8,128)S(1)}) custom-call(f32[3,1,1,8]{3,2,1,0:T(1,128)} %refs_0_.2, s32[8]{0:T(128)} %refs_1_.2, s32[8]{0:T(128)} %refs_2_.2, f32[8,6,16,256]{3,2,1,0:T(8,128)} %refs_0_.3), custom_call_target="tpu_custom_call" | custom-call | tf_op jit(solution)/shard_map/pack/pallas_call | solution.py:662
  2.5 0.2 collective-permute-start
  2.7 2.3 %collective-permute-done.refs_1_.refs_4_ = f32[8,128]{1,0:T(8,128)S(1)} collective-permute-done((f32[8,128]{1,0:T(8,128)S(1)}, f32[8,128]{1,0:T(8,128)S(1)}, u32[]{:S(2)}, u32[]{:S(2)}) %collective-permute-start) | collective-permute-done | bytes 4128 | tf_op jit(solution)/shard_map/ppermute | solution.py:598
  5.0 3.7 %collective-permute-start.1 = (f32[16,128]{1,0:T(8,128)S(1)}, f32[16,128]{1,0:T(8,128)S(1)}, u32[]{:S(2)}, u32[]{:S(2)}) collective-permute-start(f32[16,128]{1,0:T(8,128)S(1)} %pad_maximum_fusion), channel_id=1, source_target_pairs={{1,0},{2,1},{3,2},{4,3},{5,4},{6,5},{7,6},{9,8},{10,9},{11,10},{12... | collective-permute-start | bytes 24584 | tf_op jit(solution)/shard_map/ppermute | solution.py:603
  8.7 3.1 %collective-permute-start.4 = (f32[2,6,16,256]{3,2,1,0:T(8,128)S(1)}, f32[2,6,16,256]{3,2,1,0:T(8,128)S(1)}, u32[]{:S(2)}, u32[]{:S(2)}) collective-permute-start(f32[2,6,16,256]{3,2,1,0:T(8,128)S(1)} %get-tuple-element.38), channel_id=1, source_target_pairs={{0,8},{8,16},{16,24},{24,0},{1,9},{9,17},{17,25},{25,1},{2,10},{10... | collective-permute-start | bytes 589832 | tf_op jit(solution)/shard_map/ppermute | solution.py:598
  11.9 0.0 collective-permute-start.5
  11.9 1.7 %load.1 = (f32[6,16,8,256]{3,2,1,0:T(8,128)S(1)}, bf16[2,768,256]{2,1,0:T(8,128)(2,1)S(1)}, f32[24,16,256]{2,1,0:T(8,128)S(1)}) custom-call(f32[8,6,16,256]{3,2,1,0:T(8,128)} %refs_0_.3, bf16[2,768,256]{2,1,0:T(8,128)(2,1)} %constant.74.clone.refs_1_, f32[21,16,256]{2,1,0:T(8,128)} %constant.75.clone.refs_2_, f32[16,256]{1,0:T(8,128)} %refs_3_.3, ...), custom_call_target="tpu_custom_call" | custom-call | tf_op jit(solution)/shard_map/load/pallas_call | solution.py:677
  13.6 0.0 collective-permute-done.1.refs_2_
  13.6 3.4 %solve_source.1 = (f32[6,16,8,256]{3,2,1,0:T(8,128)S(1)}, f32[16,128]{1,0:T(8,128)S(1)}, f32[8,128]{1,0:T(8,128)S(1)}, f32[2,6,16,256]{3,2,1,0:T(8,128)}, f32[2,6,16,256]{3,2,1,0:T(8,128)}) custom-call(f32[8,128]{1,0:T(8,128)S(1)} %get-tuple-element.30.refs_0_, f32[8,128]{1,0:T(8,128)S(1)} %collective-permute-done.refs_1_.refs_4_, ...), custom_call_target="tpu_custom_call" | custom-call | tf_op jit(solution)/shard_map/solve_source/pallas_call | solution.py:700
  17.0 1.0 %collective-permute-start.6 = (f32[2,6,16,256]{3,2,1,0:T(8,128)}, f32[2,6,16,256]{3,2,1,0:T(8,128)S(1)}, u32[]{:S(2)}, u32[]{:S(2)}) collective-permute-start(f32[2,6,16,256]{3,2,1,0:T(8,128)} %get-tuple-element.41), channel_id=1, source_target_pairs={{0,8},{8,16},{16,24},{24,0},{1,9},{9,17},{17,25},{25,1},{2,10},{10... | collective-permute-start | bytes 589832 | tf_op jit(solution)/shard_map/ppermute | solution.py:598
  18.0 5.3 %collective-permute-start.7 = (f32[2,6,16,256]{3,2,1,0:T(8,128)}, f32[2,6,16,256]{3,2,1,0:T(8,128)S(1)}, u32[]{:S(2)}, u32[]{:S(2)}) collective-permute-start(f32[2,6,16,256]{3,2,1,0:T(8,128)} %get-tuple-element.42), channel_id=1, source_target_pairs={{0,16},{8,24},{16,0},{24,8},{1,17},{9,25},{17,1},{25,9},{2,18},{10... | collective-permute-start | bytes 589832 | tf_op jit(solution)/shard_map/ppermute | solution.py:598
  23.3 0.1 collective-permute-start.2
  23.4 13.3 %collective-permute-done.2.refs_0_.refs_4_ = f32[16,128]{1,0:T(8,128)S(1)} collective-permute-done((f32[16,128]{1,0:T(8,128)S(1)}, f32[16,128]{1,0:T(8,128)S(1)}, u32[]{:S(2)}, u32[]{:S(2)}) %collective-permute-start.2) | collective-permute-done | bytes 8224 | tf_op jit(solution)/shard_map/ppermute | solution.py:598
  36.7 0.0 collective-permute-start.3
  36.7 3.3 %collective-permute-done.3.refs_1_ = f32[8,128]{1,0:T(8,128)S(1)} collective-permute-done((f32[8,128]{1,0:T(8,128)S(1)}, f32[8,128]{1,0:T(8,128)S(1)}, u32[]{:S(2)}, u32[]{:S(2)}) %collective-permute-start.3) | collective-permute-done | bytes 4128 | tf_op jit(solution)/shard_map/ppermute | solution.py:598
  40.1 4.8 %collective-permute-start.8 = (f32[16,128]{1,0:T(8,128)S(1)}, f32[16,128]{1,0:T(8,128)S(1)}, u32[]{:S(2)}, u32[]{:S(2)}) collective-permute-start(f32[16,128]{1,0:T(8,128)S(1)} %pad_maximum_fusion.1), channel_id=1, source_target_pairs={{0,1},{1,2},{2,3},{3,4},{4,5},{5,6},{6,7},{8,9},{9,10},{10,11},{11... | collective-permute-start | bytes 24584 | tf_op jit(solution)/shard_map/ppermute | solution.py:603
  44.9 0.0 copy-start
  44.9 0.0 collective-permute-done.4.refs_2_
  44.9 0.0 collective-permute-done.5.refs_3_
  44.9 8.0 %solve_target.1 = (f32[8,6,16,256]{3,2,1,0:T(8,128)}, s32[1]{0:T(128)S(4)}, s32[12]{0:T(128)S(4)}) custom-call(f32[16,128]{1,0:T(8,128)S(1)} %collective-permute-done.2.refs_0_.refs_4_, f32[8,128]{1,0:T(8,128)S(1)} %collective-permute-done.3.refs_1_, f32[2,6,16,256]{3,2,1,0:T(8,128)S(1)} %collective-permute-done.4.refs_2_, ...), custom_call_target="tpu_custom_call" | custom-call | tf_op jit(solution)/shard_map/solve_target/pallas_call | solution.py:736
  52.9 0.0 collective-permute-done.8.refs_5_
  52.9 0.0 collective-permute-done.6.refs_1_
  52.9 0.0 collective-permute-done.7.refs_2_
  52.9 0.9 %place.1 = (f32[8,6,16,256]{3,2,1,0:T(8,128)}, f32[3,1,1,8]{3,2,1,0:T(1,128)}) custom-call(s32[12]{0:T(128)S(4)} %get-tuple-element.40.refs_0_, f32[2,6,16,256]{3,2,1,0:T(8,128)S(1)} %collective-permute-done.6.refs_1_, f32[2,6,16,256]{3,2,1,0:T(8,128)S(1)} %collective-permute-done.7.refs_2_, ...), custom_call_target="tpu_custom_call", output_to_operand_aliasing={{0}: (7, {})} | custom-call | tf_op jit(solution)/shard_map/place/pallas_call | solution.py:753
  53.8 0.0 copy-done
  (5 shorter events, 0.0 us)
Async XLA Ops:
  2.5 2.5 %collective-permute-start = (f32[8,128]{1,0:T(8,128)S(1)}, f32[8,128]{1,0:T(8,128)S(1)}, u32[]{:S(2)}, u32[]{:S(2)}) collective-permute-start(f32[8,128]{1,0:T(8,128)S(1)} %get-tuple-element.30.refs_0_), channel_id=1, source_target_pairs={{0,24},{8,0},{16,8},{24,16},{1,25},{9,1},{17,9},{25,17},{2,26},{10... | collective-permute-start | bytes 12296 | tf_op jit(solution)/shard_map/ppermute | solution.py:598
  5.0 8.6 %collective-permute-start.1 = (f32[16,128]{1,0:T(8,128)S(1)}, f32[16,128]{1,0:T(8,128)S(1)}, u32[]{:S(2)}, u32[]{:S(2)}) collective-permute-start(f32[16,128]{1,0:T(8,128)S(1)} %pad_maximum_fusion), channel_id=1, source_target_pairs={{1,0},{2,1},{3,2},{4,3},{5,4},{6,5},{7,6},{9,8},{10,9},{11,10},{12... | collective-permute-start | bytes 24584 | tf_op jit(solution)/shard_map/ppermute | solution.py:603
  8.7 36.2 %collective-permute-start.4 = (f32[2,6,16,256]{3,2,1,0:T(8,128)S(1)}, f32[2,6,16,256]{3,2,1,0:T(8,128)S(1)}, u32[]{:S(2)}, u32[]{:S(2)}) collective-permute-start(f32[2,6,16,256]{3,2,1,0:T(8,128)S(1)} %get-tuple-element.38), channel_id=1, source_target_pairs={{0,8},{8,16},{16,24},{24,0},{1,9},{9,17},{17,25},{25,1},{2,10},{10... | collective-permute-start | bytes 589832 | tf_op jit(solution)/shard_map/ppermute | solution.py:598
  11.9 33.0 %collective-permute-start.5 = (f32[2,6,16,256]{3,2,1,0:T(8,128)S(1)}, f32[2,6,16,256]{3,2,1,0:T(8,128)S(1)}, u32[]{:S(2)}, u32[]{:S(2)}) collective-permute-start(f32[2,6,16,256]{3,2,1,0:T(8,128)S(1)} %get-tuple-element.39), channel_id=1, source_target_pairs={{0,16},{8,24},{16,0},{24,8},{1,17},{9,25},{17,1},{25,9},{2,18},{10... | collective-permute-start | bytes 589832 | tf_op jit(solution)/shard_map/ppermute | solution.py:598
  17.0 35.9 %collective-permute-start.6 = (f32[2,6,16,256]{3,2,1,0:T(8,128)}, f32[2,6,16,256]{3,2,1,0:T(8,128)S(1)}, u32[]{:S(2)}, u32[]{:S(2)}) collective-permute-start(f32[2,6,16,256]{3,2,1,0:T(8,128)} %get-tuple-element.41), channel_id=1, source_target_pairs={{0,8},{8,16},{16,24},{24,0},{1,9},{9,17},{17,25},{25,1},{2,10},{10... | collective-permute-start | bytes 589832 | tf_op jit(solution)/shard_map/ppermute | solution.py:598
  18.0 34.9 %collective-permute-start.7 = (f32[2,6,16,256]{3,2,1,0:T(8,128)}, f32[2,6,16,256]{3,2,1,0:T(8,128)S(1)}, u32[]{:S(2)}, u32[]{:S(2)}) collective-permute-start(f32[2,6,16,256]{3,2,1,0:T(8,128)} %get-tuple-element.42), channel_id=1, source_target_pairs={{0,16},{8,24},{16,0},{24,8},{1,17},{9,25},{17,1},{25,9},{2,18},{10... | collective-permute-start | bytes 589832 | tf_op jit(solution)/shard_map/ppermute | solution.py:598
  23.3 13.4 %collective-permute-start.2 = (f32[16,128]{1,0:T(8,128)S(1)}, f32[16,128]{1,0:T(8,128)S(1)}, u32[]{:S(2)}, u32[]{:S(2)}) collective-permute-start(f32[16,128]{1,0:T(8,128)S(1)} %get-tuple-element.36.refs_3_), channel_id=1, source_target_pairs={{0,8},{8,16},{16,24},{24,0},{1,9},{9,17},{17,25},{25,1},{2,10},{10... | collective-permute-start | bytes 24584 | tf_op jit(solution)/shard_map/ppermute | solution.py:598
  36.7 3.4 %collective-permute-start.3 = (f32[8,128]{1,0:T(8,128)S(1)}, f32[8,128]{1,0:T(8,128)S(1)}, u32[]{:S(2)}, u32[]{:S(2)}) collective-permute-start(f32[8,128]{1,0:T(8,128)S(1)} %get-tuple-element.37), channel_id=1, source_target_pairs={{0,16},{8,24},{16,0},{24,8},{1,17},{9,25},{17,1},{25,9},{2,18},{10... | collective-permute-start | bytes 12296 | tf_op jit(solution)/shard_map/ppermute | solution.py:598
  40.1 12.8 %collective-permute-start.8 = (f32[16,128]{1,0:T(8,128)S(1)}, f32[16,128]{1,0:T(8,128)S(1)}, u32[]{:S(2)}, u32[]{:S(2)}) collective-permute-start(f32[16,128]{1,0:T(8,128)S(1)} %pad_maximum_fusion.1), channel_id=1, source_target_pairs={{0,1},{1,2},{2,3},{3,4},{4,5},{5,6},{6,7},{8,9},{9,10},{10,11},{11... | collective-permute-start | bytes 24584 | tf_op jit(solution)/shard_map/ppermute | solution.py:603
  44.9 8.9 %copy-start = (s32[8]{0:T(128)S(1)}, s32[8]{0:T(128)}, u32[]{:S(2)}) copy-start(s32[8]{0:T(128)} %refs_1_.2) | copy-start | bytes 100
